TPU v7x, 16 devices: a 4x2x1 block of a 4x4x8 slice. The times are simulated.
16 devices in a mesh: rep: 2 (over y, z), dp: 8 (over x, core).
Axes of the slice: x: 4, y: 2, z: 1, core: 2. Of those that a mesh axis runs over, the one named last changes fastest.
The devices are a block of a 4x4x8 slice.
Arguments:
- g_w_gate: bfloat16 [16, 2, 768, 6144], P(('rep', 'dp')), parts along dimension 0
- g_w_up: bfloat16 [16, 2, 768, 6144], P(('rep', 'dp')), parts along dimension 0
- g_w_down: bfloat16 [16, 2, 6144, 768], P(('rep', 'dp')), parts along dimension 0
- w_gate: bfloat16 [2, 768, 6144], replicated
- w_up: bfloat16 [2, 768, 6144], replicated
- w_down: bfloat16 [2, 6144, 768], replicated
- m_w_gate: float32 [2, 768, 6144], P(None, 'dp')
- m_w_up: float32 [2, 768, 6144], P(None, 'dp')
- m_w_down: float32 [2, 6144, 768], P(None, 'dp')
- v_w_gate: float32 [2, 768, 6144], P(None, 'dp')
- v_w_up: float32 [2, 768, 6144], P(None, 'dp')
- v_w_down: float32 [2, 6144, 768], P(None, 'dp')
Outputs:
- output 1: bfloat16 [4, 768, 6144], P('rep'), parts along dimension 0
- output 2: bfloat16 [4, 768, 6144], P('rep'), parts along dimension 0
- output 3: bfloat16 [4, 6144, 768], P('rep'), parts along dimension 0
- output 4: float32 [4, 768, 6144], P('rep', 'dp'), parts along dimension 0
- output 5: float32 [4, 768, 6144], P('rep', 'dp'), parts along dimension 0
- output 6: float32 [4, 6144, 768], P('rep', 'dp'), parts along dimension 0
- output 7: float32 [4, 768, 6144], P('rep', 'dp'), parts along dimension 0
- output 8: float32 [4, 768, 6144], P('rep', 'dp'), parts along dimension 0
- output 9: float32 [4, 6144, 768], P('rep', 'dp'), parts along dimension 0
There are 2 independent parts. A program takes and returns all parts, laid end to end along the dimension named above; an argument that names none is the same for every part.
All inputs are finite; a program needn't handle non-finite values.
Results may differ from a plain program's by a relative error of at most 0.022.
Values are sent between devices in bfloat16 or wider.
A program may use at most 768 MiB of HBM per device.

v0:
```python
import jax
import jax.numpy as jnp
from jax import lax
from jax.sharding import PartitionSpec as P


def adamw(w, m, v, g):
    m = 0.9 * m + 0.1 * g
    v = 0.95 * v + 0.05 * g * g
    step = m * lax.rsqrt(v + 1e-8) + 0.1 * w
    return (w - 0.02 * step).astype(jnp.bfloat16), m, v


def solution(mesh):
    def step(*arrays):
        terms, weights, m, v = (arrays[i : i + 3] for i in (0, 3, 6, 9))
        gradients = [lax.psum_scatter(t[0], "dp", scatter_dimension=1, tiled=True).astype(jnp.float32) for t in terms]
        me = lax.axis_index("dp")
        own = [lax.dynamic_slice_in_dim(w, me * one.shape[1], one.shape[1], 1).astype(jnp.float32) for w, one in zip(weights, m, strict=True)]
        new = [adamw(w, m, v, g) for w, m, v, g in zip(own, m, v, gradients, strict=True)]
        whole = [lax.all_gather(one[0], "dp", axis=1, tiled=True) for one in new]
        return (*whole, *(one[1] for one in new), *(one[2] for one in new))

    all_of, cut = P(None, None, None), P(None, "dp", None)
    return jax.shard_map(
        step,
        mesh=mesh,
        in_specs=(P(("rep", "dp"), None, None, None),) * 3 + (all_of,) * 3 + (cut,) * 6,
        out_specs=(P("rep", None, None),) * 3 + (P("rep", "dp", None),) * 6,
        check_vma=False,
    )
```

profile of v0, /device:TPU:113, one launch (start us, length us, event | category | flops | bytes accessed | tf_op | source)
XLA Modules:
  0.0 632.7 jit_solution(13517825249130618275)
XLA Ops:
  7.2 0.1 reduce-scatter.8.cloned.1.call-start
  7.3 0.7 reduce-scatter.8.cloned.1.call-update
  8.0 0.1 reduce-scatter.6.cloned.1.call-start
  8.1 0.7 reduce-scatter.6.cloned.1.call-update
  8.8 0.1 reduce-scatter.4.cloned.1.call-start
  8.9 0.7 reduce-scatter.4.cloned.1.call-update
  9.6 0.1 all-gather.8.cloned.1.call-start
  9.7 100.8 %reduce-scatter.8.cloned.1.call-done = bf16[2,768,768]{2,1,0:T(8,128)(2,1)} async-done(((bf16[2,6144,768]{2,1,0:T(8,128)(2,1)}), bf16[2,768,768]{2,1,0:T(8,128)(2,1)}) %reduce-scatter.8.cloned.1.call-update) | async-done | bytes 2359312 | tf_op jit(solution)/shard_map/reduce_scatter | solution.py:17
  110.5 9.6 %fusion.10 = (bf16[2,768,768]{2,1,0:T(8,128)(2,1)}, f32[2,768,768]{2,1,0:T(8,128)}, f32[2,768,768]{2,1,0:T(8,128)}) fusion(bf16[2,6144,768]{2,1,0:T(8,128)(2,1)} %param.17, s32[]{:T(128)S(6)} %select_n.8, bf16[2,768,768]{2,1,0:T(8,128)(2,1)} %reduce-scatter.8.cloned.1.call-done, f32[2,768,768]{2,1,0:T(8,128)} %param.23, f32[2,768,768]{2,1,0:T(8,128)} %param.20), kind=kLoop, calls=%fused_computation.22 | loop fusion | flops 18874368 | bytes 25952260 | tf_op jit(solution)/shard_map/convert_element_type | solution.py:11
  120.1 0.1 all-gather.8.cloned.1.call-update
  120.2 0.1 all-gather.6.cloned.1.call-start
  120.3 89.9 %reduce-scatter.6.cloned.1.call-done = bf16[2,96,6144]{2,1,0:T(8,128)(2,1)} async-done(((bf16[2,768,6144]{2,1,0:T(8,128)(2,1)}), bf16[2,96,6144]{2,1,0:T(8,128)(2,1)}) %reduce-scatter.6.cloned.1.call-update) | async-done | bytes 2359312 | tf_op jit(solution)/shard_map/reduce_scatter | solution.py:17
  210.2 9.5 %fusion.6 = (bf16[2,96,6144]{2,1,0:T(8,128)(2,1)}, f32[2,96,6144]{2,1,0:T(8,128)}, f32[2,96,6144]{2,1,0:T(8,128)}) fusion(bf16[2,768,6144]{2,1,0:T(8,128)(2,1)} %param.16, s32[]{:T(128)S(6)} %select_n.7, bf16[2,96,6144]{2,1,0:T(8,128)(2,1)} %reduce-scatter.6.cloned.1.call-done, f32[2,96,6144]{2,1,0:T(8,128)} %param.22, f32[2,96,6144]{2,1,0:T(8,128)} %param.19), kind=kLoop, calls=%fused_computation.18 | loop fusion | flops 18874368 | bytes 25952260 | tf_op jit(solution)/shard_map/convert_element_type | solution.py:11
  219.6 0.1 all-gather.6.cloned.1.call-update
  219.7 0.1 all-gather.4.cloned.1.call-start
  219.8 90.1 %reduce-scatter.4.cloned.1.call-done = bf16[2,96,6144]{2,1,0:T(8,128)(2,1)} async-done(((bf16[2,768,6144]{2,1,0:T(8,128)(2,1)}), bf16[2,96,6144]{2,1,0:T(8,128)(2,1)}) %reduce-scatter.4.cloned.1.call-update) | async-done | bytes 2359312 | tf_op jit(solution)/shard_map/reduce_scatter | solution.py:17
  309.9 9.5 %fusion.2 = (bf16[2,96,6144]{2,1,0:T(8,128)(2,1)}, f32[2,96,6144]{2,1,0:T(8,128)}, f32[2,96,6144]{2,1,0:T(8,128)}) fusion(bf16[2,768,6144]{2,1,0:T(8,128)(2,1)} %param.15, s32[]{:T(128)S(6)} %select_n.7, bf16[2,96,6144]{2,1,0:T(8,128)(2,1)} %reduce-scatter.4.cloned.1.call-done, f32[2,96,6144]{2,1,0:T(8,128)} %param.21, f32[2,96,6144]{2,1,0:T(8,128)} %param.18), kind=kLoop, calls=%fused_computation.14 | loop fusion | flops 18874368 | bytes 25952260 | tf_op jit(solution)/shard_map/convert_element_type | solution.py:11
  319.3 0.1 all-gather.4.cloned.1.call-update
  319.4 83.0 %all-gather.8.cloned.1.call-done = bf16[2,6144,768]{2,1,0:T(8,128)(2,1)} async-done(((bf16[2,768,768]{2,1,0:T(8,128)(2,1)}), bf16[2,6144,768]{2,1,0:T(8,128)(2,1)}) %all-gather.8.cloned.1.call-update) | async-done | bytes 18874384 | tf_op jit(solution)/shard_map/all_gather | solution.py:21
  402.4 92.6 %all-gather.6.cloned.1.call-done = bf16[2,768,6144]{2,1,0:T(8,128)(2,1)} async-done(((bf16[2,96,6144]{2,1,0:T(8,128)(2,1)}), bf16[2,768,6144]{2,1,0:T(8,128)(2,1)}) %all-gather.6.cloned.1.call-update) | async-done | bytes 18874384 | tf_op jit(solution)/shard_map/all_gather | solution.py:21
  495.1 92.7 %all-gather.4.cloned.1.call-done = bf16[2,768,6144]{2,1,0:T(8,128)(2,1)} async-done(((bf16[2,96,6144]{2,1,0:T(8,128)(2,1)}), bf16[2,768,6144]{2,1,0:T(8,128)(2,1)}) %all-gather.4.cloned.1.call-update) | async-done | bytes 18874384 | tf_op jit(solution)/shard_map/all_gather | solution.py:21
  587.7 0.0 copy-start
  587.7 0.0 slice-start
  587.7 20.5 %copy.24 = bf16[2,768,6144]{2,1,0:T(8,128)(2,1)} copy(bf16[2,768,6144]{2,1,0:T(8,128)(2,1)} %all-gather.4.cloned.1.call-done) | data formatting | bytes 37748736
  608.2 0.0 copy-done
  608.2 9.6 %copy.25 = bf16[2,768,6144]{2,1,0:T(8,128)(2,1)} copy(bf16[2,768,6144]{2,1,0:T(8,128)(2,1)S(1)} %copy-done) | data formatting | bytes 37748736
  617.8 0.0 slice-done
  617.8 0.0 slice-done.1
  617.8 0.0 slice-done.2
  617.8 0.0 slice-done.3
  617.8 1.2 slice-done.4
  619.0 6.8 %copy.26 = bf16[2,6144,768]{2,1,0:T(8,128)(2,1)} copy(bf16[2,6144,768]{2,1,0:T(8,128)(2,1)S(1)} %bitcast.7) | data formatting | bytes 37748736
  (5 shorter events, 0.0 us)
Async XLA Ops:
  7.2 103.3 %reduce-scatter.8.cloned.1.call-start = ((), (), s32[]{:S(2)}) async-start(), calls=%async_computation.7 | async-start | bytes 21233664 | tf_op jit(solution)/shard_map/reduce_scatter | solution.py:17
  8.0 202.2 %reduce-scatter.6.cloned.1.call-start = ((), (), s32[]{:S(2)}) async-start(), calls=%async_computation.5 | async-start | bytes 21233664 | tf_op jit(solution)/shard_map/reduce_scatter | solution.py:17
  8.8 301.1 %reduce-scatter.4.cloned.1.call-start = ((), (), s32[]{:S(2)}) async-start(), calls=%async_computation.3 | async-start | bytes 21233664 | tf_op jit(solution)/shard_map/reduce_scatter | solution.py:17
  9.6 392.8 %all-gather.8.cloned.1.call-start = ((), (), s32[]{:S(2)}) async-start(), calls=%async_computation.8 | async-start | bytes 21233664 | tf_op jit(solution)/shard_map/all_gather | solution.py:21
  120.2 374.9 %all-gather.6.cloned.1.call-start = ((), (), s32[]{:S(2)}) async-start(), calls=%async_computation.6 | async-start | bytes 21233664 | tf_op jit(solution)/shard_map/all_gather | solution.py:21
  219.7 368.0 %all-gather.4.cloned.1.call-start = ((), (), s32[]{:S(2)}) async-start(), calls=%async_computation.4 | async-start | bytes 21233664 | tf_op jit(solution)/shard_map/all_gather | solution.py:21
  587.7 20.5 %copy-start = (bf16[2,768,6144]{2,1,0:T(8,128)(2,1)S(1)}, bf16[2,768,6144]{2,1,0:T(8,128)(2,1)}, u32[]{:S(2)}) copy-start(bf16[2,768,6144]{2,1,0:T(8,128)(2,1)} %all-gather.6.cloned.1.call-done) | copy-start | bytes 56623108
  587.7 30.1 %slice-start = ((s8[18874368]{0:T(1024)(128)(4,1)}), s8[4194304]{0:T(1024)(128)(4,1)S(1)}, s32[]{:S(2)}) async-start(s8[18874368]{0:T(1024)(128)(4,1)} %bitcast.6), calls=%async_computation.9 | async-start | bytes 8388608
  587.7 30.1 %slice-start.1 = ((s8[18874368]{0:T(1024)(128)(4,1)}), s8[4194304]{0:T(1024)(128)(4,1)S(1)}, s32[]{:S(2)}) async-start(s8[18874368]{0:T(1024)(128)(4,1)} %bitcast.6), calls=%async_computation.10 | async-start | bytes 8388608
  587.7 30.1 %slice-start.2 = ((s8[18874368]{0:T(1024)(128)(4,1)}), s8[4194304]{0:T(1024)(128)(4,1)S(1)}, s32[]{:S(2)}) async-start(s8[18874368]{0:T(1024)(128)(4,1)} %bitcast.6), calls=%async_computation.11 | async-start | bytes 8388608
  608.2 9.6 %slice-start.3 = ((s8[18874368]{0:T(1024)(128)(4,1)}), s8[4194304]{0:T(1024)(128)(4,1)S(1)}, s32[]{:S(2)}) async-start(s8[18874368]{0:T(1024)(128)(4,1)} %bitcast.6), calls=%async_computation.12 | async-start | bytes 8388608
  608.2 10.8 %slice-start.4 = ((s8[18874368]{0:T(1024)(128)(4,1)}), s8[2097152]{0:T(1024)(128)(4,1)S(1)}, s32[]{:S(2)}) async-start(s8[18874368]{0:T(1024)(128)(4,1)} %bitcast.6), calls=%async_computation.13 | async-start | bytes 4194304
Sparse Core Ops, SparseCore 0:
  10.4 100.0 reduce-scatter.7
  112.8 97.2 reduce-scatter.5
  212.5 97.2 reduce-scatter.3
  311.9 90.4 all-gather.7
  404.4 90.6 all-gather.5
  497.1 90.6 all-gather.3
where the time goes:
time: 633 us
  waiting for transfers between devices  551 us (87%)
  local copies, waits for them, and re-layouts  38.2 us (6%)
  other arithmetic  28.6 us (5%)
  between operations  14.2 us (2%)
    reduce_scatter x3, waiting for transfers between devices, step(): lax.psum_scatter(t[0], 'dp', scatter_dimension=1, tiled=True)  281 us
    all_gather x3, waiting for transfers between devices, step(): whole = [lax.all_gather(one[0], 'dp', axis=1, tiled=True) for one in new]  268 us
    unnamed x15, local copies, waits for them, and re-layouts  38.2 us
    convert_element_type x3, other arithmetic, adamw(): return ((w - 0.02 * step).astype(jnp.bfloat16), m, v)  28.6 us
  transfers between devices with their start and end apart: 6, of which 6 were waited for; matrix products, arithmetic and copies ran while one was open for 5% of the time, Pallas kernels for 0%

commit v1 on v0

v1 whole, which is shorter than its diff:
```python
import functools

import jax
import jax.numpy as jnp
from jax import lax
from jax.experimental import pallas as pl
from jax.experimental.pallas import tpu as pltpu
from jax.sharding import PartitionSpec as P

MESH = pl.DeviceIdType.MESH
CORES = 2
HALVES = 2
SUB = 4
DEPTH = 4
ROWS = 16
BF16, F32 = jnp.bfloat16, jnp.float32


def adamw(w, m, v, g):
    m = 0.9 * m + 0.1 * g
    v = 0.95 * v + 0.05 * g * g
    step = m * lax.rsqrt(v + 1e-8) + 0.1 * w
    return (w - 0.02 * step).astype(jnp.bfloat16), m, v


def kernel(dims, layers, n, *refs):
    kinds = 2
    it = iter(refs)

    def take(count):
        return [next(it) for _ in range(count)]

    g, w, m, v = take(3), take(3), take(3), take(3)
    w_out, m_out, v_out = take(3), take(3), take(3)
    pair, hop1, hop2 = take(3), take(3), take(3)
    own, other, r1, r2, s1, s2, mb, vb, wb = (take(kinds) for _ in range(9))
    (pair_r, hop1_r, hop2_r, near_r, far_r, core_r) = take(6)
    (pair_s, s1_s, s2_s, near_s, relay_s, last_s) = take(6)
    (own_l, other_l, r1_l, r2_l, mvw_l, mv_w, w_w) = take(7)

    chips = n // CORES
    me = lax.axis_index("dp")
    x, c = me // CORES, me % CORES
    rx, lx, ox = (x + 1) % chips, (x + chips - 1) % chips, (x + 2) % chips
    right, left, mate = {"dp": rx * CORES + c}, {"dp": lx * CORES + c}, {"dp": x * CORES + 1 - c}

    per = layers * SUB
    total = 3 * per

    def cut(W, j):
        rows, cols = dims[W]
        if W < 2:
            width = cols // SUB
            return slice(None), pl.ds(pl.multiple_of(j * width, 128), width)
        height = rows // SUB
        return pl.ds(pl.multiple_of(j * height, 16), height), slice(None)

    def at(t, f):
        for W in range(3):

            @pl.when((t >= W * per) & (t < (W + 1) * per))
            def _():
                q = t - W * per
                f(W, W // 2, q // SUB, cut(W, q % SUB))

    def remote(src, dst, send, recv, to):
        return pltpu.make_async_remote_copy(src_ref=src, dst_ref=dst, send_sem=send, recv_sem=recv, device_id=to, device_id_type=MESH)

    def local(src, dst, sem):
        return pltpu.make_async_copy(src, dst, sem)

    def landed(ref, sem):
        local(ref, ref, sem).wait()

    def sweep(kind, body):
        height, width = s1[kind].shape[-2:]
        step = width // 3
        across = width // step

        def one(q, _):
            a, b = q // across, q % across
            body(pl.ds(pl.multiple_of(a * ROWS, ROWS), ROWS), pl.ds(pl.multiple_of(b * step, 128), step))
            return 0

        lax.fori_loop(0, (height // ROWS) * across, one, 0)


    def exchange(t):
        def go(W, k, l, p):
            remote(g[W].at[l, :, 1 - c, :, *p], pair[W].at[l, :, :, *p], pair_s.at[W], pair_r.at[t], mate).start()

        at(t, go)

    def load_own(t):
        def go(W, k, l, p):
            local(g[W].at[l, :, c, :, *p], own[k].at[t % DEPTH], own_l.at[t % DEPTH]).start()

        at(t, go)

    def load_other(t):
        def go(W, k, l, p):
            landed(pair[W].at[l, :, :, *p], pair_r.at[t])
            local(pair[W].at[l, :, :, *p], other[k].at[t % DEPTH], other_l.at[t % DEPTH]).start()

        at(t, go)

    def both(k, slot, block, half, rows, cols):
        return own[k][slot, block, half, rows, cols].astype(F32) + other[k][slot, block, half, rows, cols].astype(F32)

    def first(t):
        def go(W, k, l, p):
            slot, out = t % DEPTH, t % 2
            landed(own[k].at[slot], own_l.at[slot])
            landed(other[k].at[slot], other_l.at[slot])

            @pl.when(t >= 2)
            def _():
                landed(s1[k].at[out], s1_s.at[out])

            def add(rows, cols):
                s1[k][out, 0, rows, cols] = both(k, slot, ox, 0, rows, cols).astype(BF16)
                s1[k][out, 1, rows, cols] = both(k, slot, ox, 1, rows, cols).astype(BF16)
                s1[k][out, 2, rows, cols] = both(k, slot, rx, 1, rows, cols).astype(BF16)
                s1[k][out, 3, rows, cols] = both(k, slot, lx, 0, rows, cols).astype(BF16)

            sweep(k, add)
            remote(s1[k].at[out, 0], hop1[W].at[l, 0, *p], s1_s.at[out], hop1_r.at[t], right).start()
            remote(s1[k].at[out, 1], hop1[W].at[l, 1, *p], s1_s.at[out], hop1_r.at[t], left).start()
            remote(s1[k].at[out, 2], hop2[W].at[l, 0, 1, *p], s1_s.at[out], hop2_r.at[t], right).start()
            remote(s1[k].at[out, 3], hop2[W].at[l, 1, 0, *p], s1_s.at[out], hop2_r.at[t], left).start()

        at(t, go)

    def second(t):
        def go(W, k, l, p):
            slot, out = t % DEPTH, t % 2

            @pl.when(t >= 2)
            def _():
                landed(mb[k].at[out], mv_w.at[out, 0])
                landed(vb[k].at[out], mv_w.at[out, 1])

            local(m[W].at[l, :, *p], mb[k].at[out], mvw_l.at[out, 0]).start()
            local(v[W].at[l, :, *p], vb[k].at[out], mvw_l.at[out, 1]).start()
            local(w[W].at[l, x, c, :, *p], wb[k].at[out], mvw_l.at[out, 2]).start()
            landed(hop1[W].at[l, :, *p], hop1_r.at[t])
            local(hop1[W].at[l, :, *p], r1[k], r1_l).start()

            @pl.when(t >= 2)
            def _():
                landed(s2[k].at[out], s2_s.at[out])

            landed(r1[k], r1_l)

            def add(rows, cols):
                s2[k][out, 0, rows, cols] = (both(k, slot, rx, 0, rows, cols) + r1[k][0, rows, cols].astype(F32)).astype(BF16)
                s2[k][out, 1, rows, cols] = (both(k, slot, lx, 1, rows, cols) + r1[k][1, rows, cols].astype(F32)).astype(BF16)

            sweep(k, add)
            remote(s2[k].at[out, 0], hop2[W].at[l, 0, 0, *p], s2_s.at[out], hop2_r.at[t], right).start()
            remote(s2[k].at[out, 1], hop2[W].at[l, 1, 1, *p], s2_s.at[out], hop2_r.at[t], left).start()

        at(t, go)

    def update(t):
        def go(W, k, l, p):
            slot, out = t % DEPTH, t % 2
            landed(hop2[W].at[l, :, :, *p], hop2_r.at[t])
            local(hop2[W].at[l, :, :, *p], r2[k], r2_l).start()
            landed(mb[k].at[out], mvw_l.at[out, 0])
            landed(vb[k].at[out], mvw_l.at[out, 1])
            landed(wb[k].at[out], mvw_l.at[out, 2])
            landed(r2[k], r2_l)

            def add(rows, cols):
                for h in range(HALVES):
                    place = (out, h, rows, cols)
                    total = both(k, slot, x, h, rows, cols) + r2[k][0, h, rows, cols].astype(F32) + r2[k][1, h, rows, cols].astype(F32)
                    grad = total.astype(BF16).astype(F32)
                    wb[k][place], mb[k][place], vb[k][place] = adamw(wb[k][place].astype(F32), mb[k][place], vb[k][place], grad)

            sweep(k, add)
            mine = w_out[W].at[l, x, c, :, *p]
            local(wb[k].at[out], mine, w_w).start()
            local(mb[k].at[out], m_out[W].at[l, :, *p], mv_w.at[out, 0]).start()
            local(vb[k].at[out], v_out[W].at[l, :, *p], mv_w.at[out, 1]).start()
            landed(wb[k].at[out], w_w)
            remote(mine, mine, near_s.at[W], near_r.at[t], right).start()
            remote(mine, mine, near_s.at[W], near_r.at[t], left).start()
            remote(mine, mine, near_s.at[W], core_r.at[W], mate).start()

        at(t, go)

    def relay(t):
        def go(W, k, l, p):
            landed(hop2[W].at[l, :, :, *p], near_r.at[t])
            of_left, of_right = w_out[W].at[l, lx, c, :, *p], w_out[W].at[l, rx, c, :, *p]
            half_left, half_right = w_out[W].at[l, lx, c, 0, *p], w_out[W].at[l, rx, c, 1, *p]
            remote(half_left, half_left, relay_s.at[W], far_r.at[t], right).start()
            remote(half_right, half_right, relay_s.at[W], far_r.at[t], left).start()
            remote(of_left, of_left, last_s.at[W], core_r.at[W], mate).start()
            remote(of_right, of_right, last_s.at[W], core_r.at[W], mate).start()

        at(t, go)

    def finish(t):
        def go(W, k, l, p):
            opposite = w_out[W].at[l, ox, c, :, *p]
            landed(opposite, far_r.at[t])
            remote(opposite, opposite, last_s.at[W], core_r.at[W], mate).start()

        at(t, go)


    barrier = pltpu.get_barrier_semaphore()
    for one in (right, left, mate):
        pl.semaphore_signal(barrier, inc=1, device_id=one, device_id_type=MESH)
    pl.semaphore_wait(barrier, 3)

    exchange(0)
    load_own(0)
    exchange(1)
    load_other(0)

    def round_(i, _):
        exchange(i + 2)
        load_own(i + 1)
        first(i)
        load_other(i + 1)
        second(i - 1)
        update(i - 2)
        relay(i - 3)
        finish(i - 4)
        return 0

    lax.fori_loop(0, total + 4, round_, 0)

    for t in (total - 2, total - 1):
        landed(s1[1].at[t % 2], s1_s.at[t % 2])
        landed(s2[1].at[t % 2], s2_s.at[t % 2])
        landed(mb[1].at[t % 2], mv_w.at[t % 2, 0])
        landed(vb[1].at[t % 2], mv_w.at[t % 2, 1])
    for W in range(3):
        half_of_all = w_out[W].at[:, :, 1 - c]
        landed(half_of_all, core_r.at[W])
        landed(pair[W], pair_s.at[W])
        landed(w_out[W].at[:, pl.ds(0, 3), 0], near_s.at[W])
        landed(w_out[W].at[:, 0, 0], relay_s.at[W])
        landed(w_out[W].at[:, pl.ds(0, 3), 0], last_s.at[W])


def solution(mesh):
    n = mesh.shape["dp"]

    def step(*arrays):
        terms, weights, m, v = (arrays[i : i + 3] for i in (0, 3, 6, 9))
        layers = weights[0].shape[0]
        chips = n // CORES
        assert n == CORES * chips and chips == 4
        dims = [(one.shape[1] // HALVES, one.shape[2]) for one in m]

        def whole(one, W):
            return one.reshape(layers, chips, CORES, HALVES, *dims[W])

        def block(one, W):
            return one.reshape(layers, HALVES, *dims[W])

        inputs = (
            [whole(one, W) for W, one in enumerate(terms)]
            + [whole(one, W) for W, one in enumerate(weights)]
            + [block(one, W) for W, one in enumerate(m)]
            + [block(one, W) for W, one in enumerate(v)]
        )

        def outs(*lead, dtype=BF16):
            return [jax.ShapeDtypeStruct((*lead, *dims[W]), dtype) for W in range(3)]

        out_shape = (
            outs(layers, chips, CORES, HALVES)
            + outs(layers, HALVES, dtype=F32)
            + outs(layers, HALVES, dtype=F32)
            + outs(layers, chips, HALVES)
            + outs(layers, 2)
            + outs(layers, 2, HALVES)
        )
        tiles = [(dims[0][0], dims[0][1] // SUB), (dims[2][0] // SUB, dims[2][1])]

        def vmem(*lead, dtype=BF16):
            return [pltpu.VMEM((*lead, *tile), dtype) for tile in tiles]

        dma = pltpu.SemaphoreType.DMA
        pieces = 3 * layers * SUB
        scratch = (
            vmem(DEPTH, chips, HALVES)
            + vmem(DEPTH, chips, HALVES)
            + vmem(2)
            + vmem(2, HALVES)
            + vmem(2, 4)
            + vmem(2, 2)
            + vmem(2, HALVES, dtype=F32)
            + vmem(2, HALVES, dtype=F32)
            + vmem(2, HALVES)
            + [dma((pieces,))] * 5
            + [dma((3,))]
            + [dma((3,)), dma((2,)), dma((2,)), dma((3,)), dma((3,)), dma((3,))]
            + [dma((DEPTH,)), dma((DEPTH,)), dma, dma, dma((2, 3)), dma((2, 2)), dma]
        )
        hbm = pl.BlockSpec(memory_space=pltpu.HBM)
        result = pl.pallas_call(
            functools.partial(kernel, dims, layers, n),
            out_shape=out_shape,
            in_specs=[hbm] * len(inputs),
            out_specs=[hbm] * len(out_shape),
            scratch_shapes=scratch,
            compiler_params=pltpu.CompilerParams(collective_id=0, has_side_effects=True, vmem_limit_bytes=60 * 2**20),
            name="step",
        )(*inputs)
        like = (*weights, *m, *v)
        return tuple(one.reshape(ref.shape) for one, ref in zip(result[:9], like, strict=True))

    all_of, cut = P(None, None, None), P(None, "dp", None)
    return jax.shard_map(
        step,
        mesh=mesh,
        in_specs=(P(("rep", "dp"), None, None, None),) * 3 + (all_of,) * 3 + (cut,) * 6,
        out_specs=(P("rep", None, None),) * 3 + (P("rep", "dp", None),) * 6,
        check_vma=False,
    )
```

time: 633 us -> 531 us (0.84)
  waiting for transfers between devices: 551 us -> 0 us
  Pallas kernels: 0 us -> 469 us
  other arithmetic: 28.6 us -> 0.01 us
  local copies, waits for them, and re-layouts: 38.2 us -> 59.4 us
  between operations: 14.2 us -> 0.75 us
    pallas_call x0 -> x1, Pallas kernels: none -> 469 us  [step(): pl.pallas_call(functools.partial(kernel, dims, layers, n), out_shape=out_...]
    reduce_scatter x3 -> x0, waiting for transfers between devices: 281 us -> none  [step(): lax.psum_scatter(t[0], 'dp', scatter_dimension=1, tiled=True)]
    all_gather x3 -> x0, waiting for transfers between devices: 268 us -> none  [step(): whole = [lax.all_gather(one[0], 'dp', axis=1, tiled=True) for one in new]]
    convert_element_type x3 -> x0, other arithmetic: 28.6 us -> none  [adamw(): return ((w - 0.02 * step).astype(jnp.bfloat16), m, v)]
    unnamed x15 -> x41, local copies, waits for them, and re-layouts: 38.2 us -> 59.4 us
  transfers between devices with their start and end apart: 6 -> 0, of which waited for: 6 -> 0; matrix products, arithmetic and copies ran while one was open for 5% -> 0% of each run, Pallas kernels for 0% -> 0%
where the time goes in v1:
time: 531 us; the launch traced here: 529 us
  Pallas kernels  469 us (88%)
  local copies, waits for them, and re-layouts  59.4 us (11%)
    pallas_call x1, Pallas kernels, step(): pl.pallas_call(functools.partial(kernel, dims, layers, n), out_shape=out_...  469 us
    unnamed x41, local copies, waits for them, and re-layouts  59.4 us

profile of v1, /device:TPU:113, one launch (start us, length us, event | category | flops | bytes accessed | tf_op | source)
XLA Modules:
  0.0 528.7 jit_solution(5318712176690954234)
XLA Ops:
  0.6 468.6 %step.1 = (bf16[2,4,2,2,48,6144]{5,4,3,2,1,0:T(8,128)(2,1)}, bf16[2,4,2,2,48,6144]{5,4,3,2,1,0:T(8,128)(2,1)}, bf16[2,4,2,2,384,768]{5,4,3,2,1,0:T(8,128)(2,1)},...) custom-call(bf16[2,4,2,2,48,6144]{5,4,3,2,1,0:T(8,128)(2,1)} %bitcas, ...), custom_call_target="tpu_custom_call" | custom-call | tf_op jit(solution)/shard_map/step/pallas_call | solution.py:309
  469.2 0.0 copy-start
  469.2 0.0 slice-start
  469.2 0.0 slice-start.1
  469.2 0.0 slice-start.2
  469.2 20.5 %copy.30 = bf16[2,768,6144]{2,1,0:T(8,128)(2,1)} copy(bf16[2,768,6144]{2,1,0:T(8,128)(2,1)} %bitcast.31) | data formatting | bytes 37748736
  489.8 0.0 copy-done
  489.8 0.0 slice-start.13
  489.8 0.0 slice-start.11
  489.8 9.6 %copy.31 = bf16[2,768,6144]{2,1,0:T(8,128)(2,1)} copy(bf16[2,768,6144]{2,1,0:T(8,128)(2,1)S(1)} %bitcast.30) | data formatting | bytes 37748736
  499.3 0.0 slice-done
  499.3 0.0 slice-done.1
  499.4 0.0 slice-done.2
  499.4 0.0 slice-done.3
  499.4 1.0 slice-done.4
  500.4 8.2 %copy.32 = bf16[2,6144,768]{2,1,0:T(8,128)(2,1)} copy(bf16[2,6144,768]{2,1,0:T(8,128)(2,1)S(1)} %bitcast.29) | data formatting | bytes 37748736
  508.5 5.0 copy.33
  513.5 0.0 slice-done.13
  513.5 0.0 slice-done.14
  513.5 0.0 slice-start.7
  513.5 2.4 copy.34
  515.9 0.0 slice-done.11
  515.9 0.0 slice-done.12
  516.0 0.0 slice-start.8
  516.0 2.4 copy.35
  518.4 0.3 slice-done.9
  518.7 1.9 slice-done.10
  520.6 2.4 copy.36
  523.0 2.4 copy.37
  525.4 0.4 slice-done.5
  525.9 0.6 slice-done.6
  526.5 2.2 copy.38
  (16 shorter events, 0.0 us)
Async XLA Ops:
  469.2 20.5 %copy-start = (bf16[2,4,2,2,48,6144]{5,4,3,2,1,0:T(8,128)(2,1)S(1)}, bf16[2,4,2,2,48,6144]{5,4,3,2,1,0:T(8,128)(2,1)}, u32[]{:S(2)}) copy-start(bf16[2,4,2,2,48,6144]{5,4,3,2,1,0:T(8,128)(2,1)} %get-tuple-element.19) | copy-start | bytes 56623108
  469.2 30.1 %slice-start = ((s8[18874368]{0:T(1024)(128)(4,1)}), s8[4194304]{0:T(1024)(128)(4,1)S(1)}, s32[]{:S(2)}) async-start(s8[18874368]{0:T(1024)(128)(4,1)} %bitcast.27), calls=%async_computation | async-start | bytes 8388608
  469.2 30.1 %slice-start.1 = ((s8[18874368]{0:T(1024)(128)(4,1)}), s8[4194304]{0:T(1024)(128)(4,1)S(1)}, s32[]{:S(2)}) async-start(s8[18874368]{0:T(1024)(128)(4,1)} %bitcast.27), calls=%async_computation.1 | async-start | bytes 8388608
  469.2 30.1 %slice-start.2 = ((s8[18874368]{0:T(1024)(128)(4,1)}), s8[4194304]{0:T(1024)(128)(4,1)S(1)}, s32[]{:S(2)}) async-start(s8[18874368]{0:T(1024)(128)(4,1)} %bitcast.27), calls=%async_computation.2 | async-start | bytes 8388608
  489.8 9.6 %slice-start.3 = ((s8[18874368]{0:T(1024)(128)(4,1)}), s8[4194304]{0:T(1024)(128)(4,1)S(1)}, s32[]{:S(2)}) async-start(s8[18874368]{0:T(1024)(128)(4,1)} %bitcast.27), calls=%async_computation.3 | async-start | bytes 8388608
  489.8 10.6 %slice-start.4 = ((s8[18874368]{0:T(1024)(128)(4,1)}), s8[2097152]{0:T(1024)(128)(4,1)S(1)}, s32[]{:S(2)}) async-start(s8[18874368]{0:T(1024)(128)(4,1)} %bitcast.27), calls=%async_computation.4 | async-start | bytes 4194304
  489.8 23.8 %slice-start.13 = ((s8[4718592]{0:T(1024)(128)(4,1)}), s8[4194304]{0:T(1024)(128)(4,1)S(1)}, s32[]{:S(2)}) async-start(s8[4718592]{0:T(1024)(128)(4,1)} %bitcast.50), calls=%async_computation.13 | async-start | bytes 8388608
  489.8 26.2 %slice-start.11 = ((s8[4718592]{0:T(1024)(128)(4,1)}), s8[524288]{0:T(1024)(128)(4,1)S(1)}, s32[]{:S(2)}) async-start(s8[4718592]{0:T(1024)(128)(4,1)} %bitcast.47), calls=%async_computation.11 | async-start | bytes 1048576
  500.4 13.2 %slice-start.14 = ((s8[4718592]{0:T(1024)(128)(4,1)}), s8[524288]{0:T(1024)(128)(4,1)S(1)}, s32[]{:S(2)}) async-start(s8[4718592]{0:T(1024)(128)(4,1)} %bitcast.50), calls=%async_computation.14 | async-start | bytes 1048576
  500.4 15.6 %slice-start.12 = ((s8[4718592]{0:T(1024)(128)(4,1)}), s8[4194304]{0:T(1024)(128)(4,1)S(1)}, s32[]{:S(2)}) async-start(s8[4718592]{0:T(1024)(128)(4,1)} %bitcast.47), calls=%async_computation.12 | async-start | bytes 8388608
  513.5 5.1 slice-start.9
  513.5 9.5 %slice-start.7 = ((s8[4718592]{0:T(1024)(128)(4,1)}), s8[4194304]{0:T(1024)(128)(4,1)S(1)}, s32[]{:S(2)}) async-start(s8[4718592]{0:T(1024)(128)(4,1)} %bitcast.41), calls=%async_computation.7 | async-start | bytes 8388608
  516.0 4.7 slice-start.10
  516.0 7.1 %slice-start.8 = ((s8[4718592]{0:T(1024)(128)(4,1)}), s8[524288]{0:T(1024)(128)(4,1)S(1)}, s32[]{:S(2)}) async-start(s8[4718592]{0:T(1024)(128)(4,1)} %bitcast.41), calls=%async_computation.8 | async-start | bytes 1048576
  520.6 5.3 slice-start.5
  523.0 3.5 slice-start.6

commit v2 on v1

--- a/solution.py
+++ b/solution.py
@@ -1,4 +1,5 @@
 import functools
+import math
 
 import jax
 import jax.numpy as jnp
@@ -7,12 +8,15 @@
 from jax.experimental.pallas import tpu as pltpu
 from jax.sharding import PartitionSpec as P
 
+
 MESH = pl.DeviceIdType.MESH
 CORES = 2
 HALVES = 2
 SUB = 4
 DEPTH = 4
+LAG = 4
 ROWS = 16
+VMEM = 67_043_328
 BF16, F32 = jnp.bfloat16, jnp.float32
 
 
@@ -32,10 +36,11 @@
 
     g, w, m, v = take(3), take(3), take(3), take(3)
     w_out, m_out, v_out = take(3), take(3), take(3)
+    of_left, of_right = take(2 + layers), take(2 + layers)
     pair, hop1, hop2 = take(3), take(3), take(3)
     own, other, r1, r2, s1, s2, mb, vb, wb = (take(kinds) for _ in range(9))
-    (pair_r, hop1_r, hop2_r, near_r, far_r, core_r) = take(6)
-    (pair_s, s1_s, s2_s, near_s, relay_s, last_s) = take(6)
+    (pair_r, hop1_r, hop2_r, near_r, core_r) = take(5)
+    (pair_s, s1_s, s2_s, near_s, last_s) = take(5)
     (own_l, other_l, r1_l, r2_l, mvw_l, mv_w, w_w) = take(7)
 
     chips = n // CORES
@@ -63,6 +68,19 @@
                 q = t - W * per
                 f(W, W // 2, q // SUB, cut(W, q % SUB))
 
+    def near(t, f):
+        def go(W, k, l, p):
+            if W < 2:
+                f(W, l, p, of_left[W].at[l, *p], of_right[W].at[l, *p])
+                return
+            for layer in range(layers):
+
+                @pl.when(l == layer)
+                def _():
+                    f(W, layer, p, of_left[2 + layer].at[*p], of_right[2 + layer].at[*p])
+
+        at(t, go)
+
     def remote(src, dst, send, recv, to):
         return pltpu.make_async_remote_copy(src_ref=src, dst_ref=dst, send_sem=send, recv_sem=recv, device_id=to, device_id_type=MESH)
 
@@ -181,35 +199,34 @@
 
             sweep(k, add)
             mine = w_out[W].at[l, x, c, :, *p]
+
             local(wb[k].at[out], mine, w_w).start()
             local(mb[k].at[out], m_out[W].at[l, :, *p], mv_w.at[out, 0]).start()
             local(vb[k].at[out], v_out[W].at[l, :, *p], mv_w.at[out, 1]).start()
             landed(wb[k].at[out], w_w)
-            remote(mine, mine, near_s.at[W], near_r.at[t], right).start()
-            remote(mine, mine, near_s.at[W], near_r.at[t], left).start()
+
+        at(t, go)
+
+    def spread(t):
+        def go(W, l, p, from_left, from_right):
+            mine, first, last = w_out[W].at[l, x, c, :, *p], w_out[W].at[l, x, c, 0, *p], w_out[W].at[l, x, c, 1, *p]
+            remote(first, from_left, near_s.at[W], near_r.at[t], right).start()
+            remote(last, from_right, near_s.at[W], near_r.at[t], left).start()
+            remote(last, last, near_s.at[W], near_r.at[t], right).start()
+            remote(first, first, near_s.at[W], near_r.at[t], left).start()
             remote(mine, mine, near_s.at[W], core_r.at[W], mate).start()
 
-        at(t, go)
+        near(t, go)
 
     def relay(t):
-        def go(W, k, l, p):
+        def go(W, l, p, from_left, from_right):
             landed(hop2[W].at[l, :, :, *p], near_r.at[t])
-            of_left, of_right = w_out[W].at[l, lx, c, :, *p], w_out[W].at[l, rx, c, :, *p]
-            half_left, half_right = w_out[W].at[l, lx, c, 0, *p], w_out[W].at[l, rx, c, 1, *p]
-            remote(half_left, half_left, relay_s.at[W], far_r.at[t], right).start()
-            remote(half_right, half_right, relay_s.at[W], far_r.at[t], left).start()
-            remote(of_left, of_left, last_s.at[W], core_r.at[W], mate).start()
-            remote(of_right, of_right, last_s.at[W], core_r.at[W], mate).start()
-
-        at(t, go)
-
-    def finish(t):
-        def go(W, k, l, p):
-            opposite = w_out[W].at[l, ox, c, :, *p]
-            landed(opposite, far_r.at[t])
-            remote(opposite, opposite, last_s.at[W], core_r.at[W], mate).start()
-
-        at(t, go)
+            left0, left1 = w_out[W].at[l, lx, c, 0, *p], w_out[W].at[l, lx, c, 1, *p]
+            right0, right1 = w_out[W].at[l, rx, c, 0, *p], w_out[W].at[l, rx, c, 1, *p]
+            for src, dst in ((from_left, left0), (left1, left1), (right0, right0), (from_right, right1)):
+                remote(src, dst, last_s.at[W], core_r.at[W], mate).start()
+
+        near(t, go)
 
 
     barrier = pltpu.get_barrier_semaphore()
@@ -229,11 +246,11 @@
         load_other(i + 1)
         second(i - 1)
         update(i - 2)
-        relay(i - 3)
-        finish(i - 4)
+        spread(i - 2 - LAG)
+        relay(i - 3 - LAG)
         return 0
 
-    lax.fori_loop(0, total + 4, round_, 0)
+    lax.fori_loop(0, total + 3 + LAG, round_, 0)
 
     for t in (total - 2, total - 1):
         landed(s1[1].at[t % 2], s1_s.at[t % 2])
@@ -241,18 +258,66 @@
         landed(mb[1].at[t % 2], mv_w.at[t % 2, 0])
         landed(vb[1].at[t % 2], mv_w.at[t % 2, 1])
     for W in range(3):
-        half_of_all = w_out[W].at[:, :, 1 - c]
-        landed(half_of_all, core_r.at[W])
+        landed(w_out[W].at[:, pl.ds(0, 3), 0], core_r.at[W])
         landed(pair[W], pair_s.at[W])
         landed(w_out[W].at[:, pl.ds(0, 3), 0], near_s.at[W])
-        landed(w_out[W].at[:, 0, 0], relay_s.at[W])
-        landed(w_out[W].at[:, pl.ds(0, 3), 0], last_s.at[W])
+        landed(w_out[W].at[:, pl.ds(0, 2), 0], last_s.at[W])
+
+
+def moves(sources, results, jobs, given=None):
+    count, extra = len(sources), 0 if given is None else 1
+
+    def body(*refs):
+        ins, outs = refs[:count], refs[count + extra : count + extra + len(results)]
+        bufs, (got, put) = refs[count + extra + len(results) : -2], refs[-2:]
+        me = lax.axis_index("dp")
+        x, c = me // CORES, me % CORES
+
+        def load(q, i):
+            src, _, _, slots, _, _, where = jobs[q]
+            return pltpu.make_async_copy(ins[src].at[where(i, x, c)[0]], bufs[q].at[i % slots], got.at[q, i % slots])
+
+        def store(q, i):
+            _, dst, _, slots, _, _, where = jobs[q]
+            return pltpu.make_async_copy(bufs[q].at[i % slots], outs[dst].at[where(i, x, c)[1]], put.at[q, i % slots])
+
+        for i in range(max(job[4] for job in jobs)):
+            for q, job in enumerate(jobs):
+                if i < min(job[4], job[2]):
+                    load(q, i).start()
+        for i in range(max(job[2] for job in jobs)):
+            for q, (_, _, steps, slots, ahead, _, _) in enumerate(jobs):
+                if i < steps:
+                    load(q, i).wait()
+                    store(q, i).start()
+                    if i + ahead < steps:
+                        if i + ahead >= slots:
+                            store(q, i + ahead - slots).wait()
+                        load(q, i + ahead).start()
+        for q, (_, _, steps, slots, _, _, _) in enumerate(jobs):
+            for i in range(max(0, steps - slots), steps):
+                store(q, i).wait()
+
+    most = max(job[3] for job in jobs)
+    hbm = pl.BlockSpec(memory_space=pltpu.HBM)
+    nbytes = 2 * sum(job[2] * math.prod(job[5]) * sources[job[0]].dtype.itemsize for job in jobs)
+    return pl.pallas_call(
+        body,
+        in_specs=[hbm] * (count + extra),
+        out_specs=[hbm] * len(results),
+        out_shape=results,
+        scratch_shapes=[pltpu.VMEM((job[3], *job[5]), sources[job[0]].dtype) for job in jobs]
+        + [pltpu.SemaphoreType.DMA((len(jobs), most))] * 2,
+        input_output_aliases={count: 0} if extra else {},
+        compiler_params=pltpu.CompilerParams(vmem_limit_bytes=VMEM),
+        cost_estimate=pl.CostEstimate(flops=nbytes * 8, bytes_accessed=nbytes, transcendentals=0),
+    )(*sources, *(() if given is None else (given,)))
 
 
 def solution(mesh):
     n = mesh.shape["dp"]
 
-    def step(*arrays):
+    def update(*arrays):
         terms, weights, m, v = (arrays[i : i + 3] for i in (0, 3, 6, 9))
         layers = weights[0].shape[0]
         chips = n // CORES
@@ -275,10 +340,12 @@
         def outs(*lead, dtype=BF16):
             return [jax.ShapeDtypeStruct((*lead, *dims[W]), dtype) for W in range(3)]
 
+        nears = outs(layers)[:2] + [jax.ShapeDtypeStruct(dims[2], BF16)] * layers
         out_shape = (
             outs(layers, chips, CORES, HALVES)
             + outs(layers, HALVES, dtype=F32)
             + outs(layers, HALVES, dtype=F32)
+            + nears * 2
             + outs(layers, chips, HALVES)
             + outs(layers, 2)
             + outs(layers, 2, HALVES)
@@ -300,9 +367,9 @@
             + vmem(2, HALVES, dtype=F32)
             + vmem(2, HALVES, dtype=F32)
             + vmem(2, HALVES)
-            + [dma((pieces,))] * 5
+            + [dma((pieces,))] * 4
             + [dma((3,))]
-            + [dma((3,)), dma((2,)), dma((2,)), dma((3,)), dma((3,)), dma((3,))]
+            + [dma((3,)), dma((2,)), dma((2,)), dma((3,)), dma((3,))]
             + [dma((DEPTH,)), dma((DEPTH,)), dma, dma, dma((2, 3)), dma((2, 2)), dma]
         )
         hbm = pl.BlockSpec(memory_space=pltpu.HBM)
@@ -312,15 +379,109 @@
             in_specs=[hbm] * len(inputs),
             out_specs=[hbm] * len(out_shape),
             scratch_shapes=scratch,
-            compiler_params=pltpu.CompilerParams(collective_id=0, has_side_effects=True, vmem_limit_bytes=60 * 2**20),
+            compiler_params=pltpu.CompilerParams(collective_id=0, has_side_effects=True, vmem_limit_bytes=VMEM),
             name="step",
         )(*inputs)
-        like = (*weights, *m, *v)
-        return tuple(one.reshape(ref.shape) for one, ref in zip(result[:9], like, strict=True))
+        new_w, new_m, new_v = result[:3], result[3:6], result[6:9]
+        of_left, of_right = result[9 : 9 + len(nears)], result[9 + len(nears) : 9 + 2 * len(nears)]
+
+        def moved(one, along, other=False):
+            to = [((d // CORES + along) % chips * CORES + (d % CORES + other) % CORES) for d in range(n)]
+            return lax.ppermute(one, "dp", list(enumerate(to)))
+
+        def like(one):
+            return jax.ShapeDtypeStruct(one.shape, one.dtype)
+
+        every = slice(None)
+
+        def of_blocks(W, src, dst, blocks, half, slots, ahead):
+            def where(i, x, c):
+                along, other, which = blocks[i // layers]
+                place = (i % layers, (x + along) % chips, 1 - c if other else c, which)
+                return place, place
+
+            return src, dst, layers * len(blocks), slots, ahead, dims[W] if half else (HALVES, *dims[W]), where
+
+        def of_near(W, src, dst, along, other, half, layer=None, slots=2):
+            cuts = 2
+            shape = (dims[W][0], dims[W][1] // cuts) if W < 2 else (dims[W][0] // cuts, dims[W][1])
+
+            def where(i, x, c):
+                q = i % cuts
+                at = (every, pl.ds(q * shape[1], shape[1])) if W < 2 else (pl.ds(q * shape[0], shape[0]), every)
+                l = i // cuts if layer is None else layer
+                return ((l, *at) if layer is None else at), (l, (x + along) % chips, 1 - c if other else c, half, *at)
+
+            steps = cuts * (layers if layer is None else 1)
+            return src, dst, steps, slots, slots // 2, shape, where
+
+        def of_moment(W, src, dst, cuts, slots, ahead):
+            shape = (dims[W][0], dims[W][1] // cuts) if W < 2 else (dims[W][0] // cuts, dims[W][1])
+
+            def where(i, x, c):
+                q = i % cuts
+                at = (every, pl.ds(q * shape[1], shape[1])) if W < 2 else (pl.ds(q * shape[0], shape[0]), every)
+                place = (i // (cuts * HALVES), i // cuts % HALVES, *at)
+                return place, place
+
+            return src, dst, layers * HALVES * cuts, slots, ahead, shape, where
+
+        def copied(which, new_w, new_m, new_v, of_left, of_right):
+            here = [one[W] for one in (new_w, new_m, new_v) for W in which]
+            count, jobs, late = len(which), [], []
+            for q, W in enumerate(which):
+                full = ((0, False, every), (0, True, every), (-1, True, every), (1, True, every))
+                jobs.append(of_blocks(W, q, q, full, False, 6, 3))
+                jobs.append(of_blocks(W, q, q, ((-1, False, 1), (1, False, 0)), True, 4, 2))
+                jobs += [of_moment(W, i, i, 2, 6, 3) for i in (count + q, 2 * count + q)]
+                for layer in (None,) if W < 2 else range(layers):
+                    at = W + (layer or 0)
+                    for one, along, half in ((of_left, -1, 0), (of_right, 1, 1)):
+                        jobs.append(of_near(W, len(here) + len(late), q, along, False, half, layer, 4))
+                        late.append(one[at])
+            return moves((*here, *late), [like(one) for one in here], jobs)
+
+        def placed(W, one, halves):
+            jobs = [of_near(W, i, 0, 2, other, half, layer, 4) for i, (_, other, half, layer) in enumerate(halves)]
+            return moves([half[0] for half in halves], [like(one)], jobs, one)[0]
+
+        def over(far):
+            return [moved(one, 0, True) for one in far]
+
+        def halves(far, mates, layer=None):
+            return [(one, other, h, layer) for other, both in ((False, far), (True, mates)) for h, one in enumerate(both)]
+
+        def after(far, which, *others):
+            one, others = lax.optimization_barrier((far[which], others))
+            return [one if i == which else old for i, old in enumerate(far)], *others
+
+        far = []
+        for a, b in zip(of_left, of_right, strict=True):
+            far.append((moved(a, 1), moved(b, -1)))
+        gate, up, gate_m, up_m, gate_v, up_v = copied((0, 1), new_w, new_m, new_v, of_left, of_right)
+        far, _, *rest = after(far, 0, gate_m, new_w, new_m, new_v, of_left, of_right)
+        gate_mate = over(far[0])
+        down, down_m, down_v = copied((2,), *rest)
+        far, gate_mate, _ = after(far, 1, gate_mate, down_m)
+        up_mate = over(far[1])
+        gate = placed(0, gate, halves(far[0], gate_mate))
+        far, up_mate, gate = after(far, 2, up_mate, gate)
+        down_mate = over(far[2])
+        up = placed(1, up, halves(far[1], up_mate))
+        for layer in range(1, layers):
+            far, down_mate, up = after(far, 2 + layer, down_mate, up)
+            next_mate = over(far[2 + layer])
+            down = placed(2, down, halves(far[1 + layer], down_mate, layer - 1))
+            down_mate = next_mate
+        down = placed(2, down, halves(far[1 + layers], (), layers - 1))
+        down = placed(2, down, [(one, True, h, layers - 1) for h, one in enumerate(down_mate)])
+
+        found = (gate, up, down, gate_m, up_m, down_m, gate_v, up_v, down_v)
+        return tuple(one.reshape(ref.shape) for one, ref in zip(found, (*weights, *m, *v), strict=True))
 
     all_of, cut = P(None, None, None), P(None, "dp", None)
     return jax.shard_map(
-        step,
+        update,
         mesh=mesh,
         in_specs=(P(("rep", "dp"), None, None, None),) * 3 + (all_of,) * 3 + (cut,) * 6,
         out_specs=(P("rep", None, None),) * 3 + (P("rep", "dp", None),) * 6,

time: 531 us -> 492 us (0.927)
  local copies, waits for them, and re-layouts: 59.4 us -> 0 us
  starting transfers between devices: 0 us -> 16.3 us
  waiting for transfers between devices: 0 us -> 14 us
  Pallas kernels: 469 us -> 459 us
    unnamed x41 -> x0, local copies, waits for them, and re-layouts: 59.4 us -> none
    ppermute x0 -> x16, starting transfers between devices: none -> 16.3 us  [moved(): return lax.ppermute(one, 'dp', list(enumerate(to)))]
    ppermute x0 -> x16, waiting for transfers between devices: none -> 14 us  [moved(): return lax.ppermute(one, 'dp', list(enumerate(to)))]
    pallas_call x1 -> x8, Pallas kernels: 469 us -> 459 us  [the longest x1 394 us: update(): pl.pallas_call(functools.partial(kernel, dims, layers, n), out_shape=out_...]
  transfers between devices with their start and end apart: 0 -> 16, of which waited for: 0 -> 3; matrix products, arithmetic and copies ran while one was open for 0% -> 0% of each run, Pallas kernels for 0% -> 13%
where the time goes in v2:
time: 492 us; the launch traced here: 490 us
  Pallas kernels  459 us (93%)
  starting transfers between devices  16.3 us (3%)
  waiting for transfers between devices  14 us (3%)
    pallas_call x1, Pallas kernels, update(): pl.pallas_call(functools.partial(kernel, dims, layers, n), out_shape=out_...  394 us
    pallas_call x7, Pallas kernels, moves(): pl.pallas_call(body, in_specs=[hbm] * (count + extra), out_specs=[hbm] *...  64.9 us
    ppermute x16, starting transfers between devices, moved(): return lax.ppermute(one, 'dp', list(enumerate(to)))  16.3 us
    ppermute x16, waiting for transfers between devices, moved(): return lax.ppermute(one, 'dp', list(enumerate(to)))  14 us
  transfers between devices with their start and end apart: 16, of which 3 were waited for; matrix products, arithmetic and copies ran while one was open for 0% of the time, Pallas kernels for 13%

profile of v2, /device:TPU:113, one launch (start us, length us, event | category | flops | bytes accessed | tf_op | source)
XLA Modules:
  0.0 489.9 jit_solution(17842708541834434485)
XLA Ops:
  0.6 393.9 %step.1 = (bf16[2,4,2,2,48,6144]{5,4,3,2,1,0:T(8,128)(2,1)}, bf16[2,4,2,2,48,6144]{5,4,3,2,1,0:T(8,128)(2,1)}, bf16[2,4,2,2,384,768]{5,4,3,2,1,0:T(8,128)(2,1)},...) custom-call(bf16[2,4,2,2,48,6144]{5,4,3,2,1,0:T(8,128)(2,1)} %bitcas, ...), custom_call_target="tpu_custom_call" | custom-call | tf_op jit(solution)/shard_map/step/pallas_call | solution.py:376
  394.6 0.1 collective-permute-start.4
  394.7 2.6 collective-permute-start.5
  397.3 0.0 collective-permute-start.2
  397.3 2.7 collective-permute-start.3
  400.0 32.0 %shard_map.187 = (bf16[2,4,2,2,48,6144]{5,4,3,2,1,0:T(8,128)(2,1)}, bf16[2,4,2,2,48,6144]{5,4,3,2,1,0:T(8,128)(2,1)}, f32[2,2,48,6144]{3,2,1,0:T(8,128)}, f32[2,...) custom-call(bf16[2,4,2,2,48,6144]{5,4,3,2,1,0:T(8,128)(2,1)} %get-tuple-element.64.refs_0_, ...), custom_call_target="tpu_custom_call" | custom-call | flops 754974720 | bytes 94371840 | tf_op jit(solution)/shard_map/pallas_call | solution.py:304
  432.0 0.0 collective-permute-done.4.refs_0_
  432.0 1.3 collective-permute-start.6
  433.4 0.1 collective-permute-start.7
  433.5 16.8 %shard_map.188 = (bf16[2,4,2,2,384,768]{5,4,3,2,1,0:T(8,128)(2,1)}, f32[2,2,384,768]{3,2,1,0:T(8,128)}, f32[2,2,384,768]{3,2,1,0:T(8,128)}) custom-call(bf16[2,4,2,2,384,768]{5,4,3,2,1,0:T(8,128)(2,1)} %get-tuple-element.78.refs_0_, f32[2,2,384,768]{3,2,1,0:T(8,128)} %get-tuple-element.79.refs_1_, f32[2,2,384,768]{3,2,1,0:T(8,128)} %get-tuple-element.80.refs_2_, ...), custom_call_target="tpu_custom_call" | custom-call | flops 377487360 | bytes 47185920 | tf_op jit(solution)/shard_map/pallas_call | solution.py:304
  450.3 0.0 collective-permute-done.2.refs_0_
  450.3 0.0 collective-permute-done.6.refs_2_
  450.3 0.0 collective-permute-done.7.refs_3_
  450.3 0.5 collective-permute-start.8
  450.8 0.1 collective-permute-start.9
  450.9 2.7 collective-permute-start.1
  453.6 0.0 collective-permute-start.10
  453.6 4.6 shard_map.189
  458.2 8.7 %collective-permute-done.refs_0_ = bf16[384,768]{1,0:T(8,128)(2,1)} collective-permute-done((bf16[384,768]{1,0:T(8,128)(2,1)}, bf16[384,768]{1,0:T(8,128)(2,1)}, u32[]{:S(2)}, u32[]{:S(2)}) %collective-permute-start) | collective-permute-done | bytes 589856 | tf_op jit(solution)/shard_map/ppermute | solution.py:390
  466.9 0.5 collective-permute-start.11
  467.4 0.0 collective-permute-done.1.refs_1_
  467.4 0.0 collective-permute-done.8.refs_2_
  467.4 2.5 collective-permute-start.12
  469.9 0.1 collective-permute-start.13
  470.0 4.6 shard_map.190
  474.6 4.9 collective-permute-done.10.refs_0_
  479.5 0.4 collective-permute-done.11.refs_1_
  480.0 3.0 collective-permute-start.14
  483.0 0.1 collective-permute-start.15
  483.0 2.6 shard_map.191.refs_2_
  485.7 2.1 shard_map.192.refs_2_
  487.8 2.1 shard_map.193
  (8 shorter events, 0.0 us)
Async XLA Ops:
  394.6 37.4 %collective-permute-start.4 = (bf16[2,48,6144]{2,1,0:T(8,128)(2,1)}, bf16[2,48,6144]{2,1,0:T(8,128)(2,1)}, u32[]{:S(2)}, u32[]{:S(2)}) collective-permute-start(bf16[2,48,6144]{2,1,0:T(8,128)(2,1)} %get-tuple-element.62.refs_6_), channel_id=1, source_target_pairs={{0,2},{1,3},{2,4},{3,5},{4,6},{5,7},{6,0},{7,1},{8,10},{9,11},{10,... | collective-permute-start | bytes 3538952 | tf_op jit(solution)/shard_map/ppermute | solution.py:390
  394.7 37.3 %collective-permute-start.5 = (bf16[2,48,6144]{2,1,0:T(8,128)(2,1)}, bf16[2,48,6144]{2,1,0:T(8,128)(2,1)}, u32[]{:S(2)}, u32[]{:S(2)}) collective-permute-start(bf16[2,48,6144]{2,1,0:T(8,128)(2,1)} %get-tuple-element.63.refs_7_), channel_id=1, source_target_pairs={{0,6},{1,7},{2,0},{3,1},{4,2},{5,3},{6,4},{7,5},{8,14},{9,15},{10,... | collective-permute-start | bytes 3538952 | tf_op jit(solution)/shard_map/ppermute | solution.py:390
  397.3 52.9 %collective-permute-start.2 = (bf16[2,48,6144]{2,1,0:T(8,128)(2,1)}, bf16[2,48,6144]{2,1,0:T(8,128)(2,1)}, u32[]{:S(2)}, u32[]{:S(2)}) collective-permute-start(bf16[2,48,6144]{2,1,0:T(8,128)(2,1)} %get-tuple-element.60.refs_8_), channel_id=1, source_target_pairs={{0,2},{1,3},{2,4},{3,5},{4,6},{5,7},{6,0},{7,1},{8,10},{9,11},{10,... | collective-permute-start | bytes 3538952 | tf_op jit(solution)/shard_map/ppermute | solution.py:390
  397.3 52.9 %collective-permute-start.3 = (bf16[2,48,6144]{2,1,0:T(8,128)(2,1)}, bf16[2,48,6144]{2,1,0:T(8,128)(2,1)}, u32[]{:S(2)}, u32[]{:S(2)}) collective-permute-start(bf16[2,48,6144]{2,1,0:T(8,128)(2,1)} %get-tuple-element.61.refs_9_), channel_id=1, source_target_pairs={{0,6},{1,7},{2,0},{3,1},{4,2},{5,3},{6,4},{7,5},{8,14},{9,15},{10,... | collective-permute-start | bytes 3538952 | tf_op jit(solution)/shard_map/ppermute | solution.py:390
  432.0 18.3 %collective-permute-start.6 = (bf16[2,48,6144]{2,1,0:T(8,128)(2,1)}, bf16[2,48,6144]{2,1,0:T(8,128)(2,1)}, u32[]{:S(2)}, u32[]{:S(2)}) collective-permute-start(bf16[2,48,6144]{2,1,0:T(8,128)(2,1)} %collective-permute-done.4.refs_0_), channel_id=1, source_target_pairs={{0,1},{1,0},{2,3},{3,2},{4,5},{5,4},{6,7},{7,6},{8,9},{9,8},{10,11... | collective-permute-start | bytes 3538952 | tf_op jit(solution)/shard_map/ppermute | solution.py:390
  433.4 16.9 %collective-permute-start.7 = (bf16[2,48,6144]{2,1,0:T(8,128)(2,1)}, bf16[2,48,6144]{2,1,0:T(8,128)(2,1)}, u32[]{:S(2)}, u32[]{:S(2)}) collective-permute-start(bf16[2,48,6144]{2,1,0:T(8,128)(2,1)} %collective-permute-done.5.refs_1_), channel_id=1, source_target_pairs={{0,1},{1,0},{2,3},{3,2},{4,5},{5,4},{6,7},{7,6},{8,9},{9,8},{10,11... | collective-permute-start | bytes 3538952 | tf_op jit(solution)/shard_map/ppermute | solution.py:390
  450.3 17.1 %collective-permute-start.8 = (bf16[2,48,6144]{2,1,0:T(8,128)(2,1)}, bf16[2,48,6144]{2,1,0:T(8,128)(2,1)}, u32[]{:S(2)}, u32[]{:S(2)}) collective-permute-start(bf16[2,48,6144]{2,1,0:T(8,128)(2,1)} %collective-permute-done.2.refs_0_), channel_id=1, source_target_pairs={{0,1},{1,0},{2,3},{3,2},{4,5},{5,4},{6,7},{7,6},{8,9},{9,8},{10,11... | collective-permute-start | bytes 3538952 | tf_op jit(solution)/shard_map/ppermute | solution.py:390
  450.8 16.6 %collective-permute-start.9 = (bf16[2,48,6144]{2,1,0:T(8,128)(2,1)}, bf16[2,48,6144]{2,1,0:T(8,128)(2,1)}, u32[]{:S(2)}, u32[]{:S(2)}) collective-permute-start(bf16[2,48,6144]{2,1,0:T(8,128)(2,1)} %collective-permute-done.3.refs_1_), channel_id=1, source_target_pairs={{0,1},{1,0},{2,3},{3,2},{4,5},{5,4},{6,7},{7,6},{8,9},{9,8},{10,11... | collective-permute-start | bytes 3538952 | tf_op jit(solution)/shard_map/ppermute | solution.py:390
  450.9 16.0 %collective-permute-start = (bf16[384,768]{1,0:T(8,128)(2,1)}, bf16[384,768]{1,0:T(8,128)(2,1)}, u32[]{:S(2)}, u32[]{:S(2)}) collective-permute-start(bf16[384,768]{1,0:T(8,128)(2,1)} %get-tuple-element.81.refs_3_), channel_id=1, source_target_pairs={{0,2},{1,3},{2,4},{3,5},{4,6},{5,7},{6,0},{7,1},{8,10},{9,11},{10,... | collective-permute-start | bytes 1769480 | tf_op jit(solution)/shard_map/ppermute | solution.py:390
  450.9 16.5 %collective-permute-start.1 = (bf16[384,768]{1,0:T(8,128)(2,1)}, bf16[384,768]{1,0:T(8,128)(2,1)}, u32[]{:S(2)}, u32[]{:S(2)}) collective-permute-start(bf16[384,768]{1,0:T(8,128)(2,1)} %get-tuple-element.82.refs_4_), channel_id=1, source_target_pairs={{0,6},{1,7},{2,0},{3,1},{4,2},{5,3},{6,4},{7,5},{8,14},{9,15},{10,... | collective-permute-start | bytes 1769480 | tf_op jit(solution)/shard_map/ppermute | solution.py:390
  453.6 26.0 %collective-permute-start.10 = (bf16[384,768]{1,0:T(8,128)(2,1)}, bf16[384,768]{1,0:T(8,128)(2,1)}, u32[]{:S(2)}, u32[]{:S(2)}) collective-permute-start(bf16[384,768]{1,0:T(8,128)(2,1)} %get-tuple-element.83.refs_5_), channel_id=1, source_target_pairs={{0,2},{1,3},{2,4},{3,5},{4,6},{5,7},{6,0},{7,1},{8,10},{9,11},{10,... | collective-permute-start | bytes 1769480 | tf_op jit(solution)/shard_map/ppermute | solution.py:390
  466.9 13.1 %collective-permute-start.11 = (bf16[384,768]{1,0:T(8,128)(2,1)}, bf16[384,768]{1,0:T(8,128)(2,1)}, u32[]{:S(2)}, u32[]{:S(2)}) collective-permute-start(bf16[384,768]{1,0:T(8,128)(2,1)} %get-tuple-element.84.refs_6_), channel_id=1, source_target_pairs={{0,6},{1,7},{2,0},{3,1},{4,2},{5,3},{6,4},{7,5},{8,14},{9,15},{10,... | collective-permute-start | bytes 1769480 | tf_op jit(solution)/shard_map/ppermute | solution.py:390
  467.4 12.5 %collective-permute-start.12 = (bf16[384,768]{1,0:T(8,128)(2,1)}, bf16[384,768]{1,0:T(8,128)(2,1)}, u32[]{:S(2)}, u32[]{:S(2)}) collective-permute-start(bf16[384,768]{1,0:T(8,128)(2,1)} %collective-permute-done.refs_0_), channel_id=1, source_target_pairs={{0,1},{1,0},{2,3},{3,2},{4,5},{5,4},{6,7},{7,6},{8,9},{9,8},{10,11... | collective-permute-start | bytes 1769480 | tf_op jit(solution)/shard_map/ppermute | solution.py:390
  469.9 10.0 %collective-permute-start.13 = (bf16[384,768]{1,0:T(8,128)(2,1)}, bf16[384,768]{1,0:T(8,128)(2,1)}, u32[]{:S(2)}, u32[]{:S(2)}) collective-permute-start(bf16[384,768]{1,0:T(8,128)(2,1)} %collective-permute-done.1.refs_1_), channel_id=1, source_target_pairs={{0,1},{1,0},{2,3},{3,2},{4,5},{5,4},{6,7},{7,6},{8,9},{9,8},{10,11... | collective-permute-start | bytes 1769480 | tf_op jit(solution)/shard_map/ppermute | solution.py:390
  480.0 7.9 %collective-permute-start.14 = (bf16[384,768]{1,0:T(8,128)(2,1)}, bf16[384,768]{1,0:T(8,128)(2,1)}, u32[]{:S(2)}, u32[]{:S(2)}) collective-permute-start(bf16[384,768]{1,0:T(8,128)(2,1)} %collective-permute-done.10.refs_0_), channel_id=1, source_target_pairs={{0,1},{1,0},{2,3},{3,2},{4,5},{5,4},{6,7},{7,6},{8,9},{9,8},{10,11... | collective-permute-start | bytes 1769480 | tf_op jit(solution)/shard_map/ppermute | solution.py:390
  483.0 4.9 collective-permute-start.15

commit v3 on v2

--- a/solution.py
+++ b/solution.py
@@ -39,7 +39,7 @@
     of_left, of_right = take(2 + layers), take(2 + layers)
     pair, hop1, hop2 = take(3), take(3), take(3)
     own, other, r1, r2, s1, s2, mb, vb, wb = (take(kinds) for _ in range(9))
-    (pair_r, hop1_r, hop2_r, near_r, core_r) = take(5)
+    (pair_r, hop1_r, hop2_r, near_r, core_r, open_r) = take(6)
     (pair_s, s1_s, s2_s, near_s, last_s) = take(5)
     (own_l, other_l, r1_l, r2_l, mvw_l, mv_w, w_w) = take(7)
 
@@ -124,6 +124,30 @@
 
     def both(k, slot, block, half, rows, cols):
         return own[k][slot, block, half, rows, cols].astype(F32) + other[k][slot, block, half, rows, cols].astype(F32)
+
+    def opening():
+        p = cut(0, 0)
+        blocks = ((ox, (0, 1)), (rx, (2,)), (lx, (3,)), (x, ()))
+        for i, (block, _) in enumerate(blocks):
+            remote(g[0].at[0, block, 1 - c, :, *p], other[0].at[0, block], pair_s.at[0], open_r.at[i], mate).start()
+        exchange(1)
+        exchange(2)
+        load_own(1)
+        landed(own[0].at[0], own_l.at[0])
+        halves = ((ox, 0), (ox, 1), (rx, 1), (lx, 0))
+        ends = ((hop1, (0,), hop1_r, right), (hop1, (1,), hop1_r, left), (hop2, (0, 1), hop2_r, right), (hop2, (1, 0), hop2_r, left))
+        for i, (block, which) in enumerate(blocks):
+            landed(other[0].at[0, block], open_r.at[i])
+            if which:
+
+                def add(rows, cols):
+                    for q in which:
+                        s1[0][0, q, rows, cols] = both(0, 0, *halves[q], rows, cols).astype(BF16)
+
+                sweep(0, add)
+            for q in which:
+                hop, place, sem, to = ends[q]
+                remote(s1[0].at[0, q], hop[0].at[0, *place, *p], s1_s.at[0], sem.at[0], to).start()
 
     def first(t):
         def go(W, k, l, p):
@@ -229,15 +253,14 @@
         near(t, go)
 
 
+    load_own(0)
     barrier = pltpu.get_barrier_semaphore()
     for one in (right, left, mate):
         pl.semaphore_signal(barrier, inc=1, device_id=one, device_id_type=MESH)
     pl.semaphore_wait(barrier, 3)
 
-    exchange(0)
-    load_own(0)
-    exchange(1)
-    load_other(0)
+    opening()
+    load_other(1)
 
     def round_(i, _):
         exchange(i + 2)
@@ -250,7 +273,7 @@
         relay(i - 3 - LAG)
         return 0
 
-    lax.fori_loop(0, total + 3 + LAG, round_, 0)
+    lax.fori_loop(1, total + 3 + LAG, round_, 0)
 
     for t in (total - 2, total - 1):
         landed(s1[1].at[t % 2], s1_s.at[t % 2])
@@ -368,7 +391,7 @@
             + vmem(2, HALVES, dtype=F32)
             + vmem(2, HALVES)
             + [dma((pieces,))] * 4
-            + [dma((3,))]
+            + [dma((3,)), dma((chips,))]
             + [dma((3,)), dma((2,)), dma((2,)), dma((3,)), dma((3,))]
             + [dma((DEPTH,)), dma((DEPTH,)), dma, dma, dma((2, 3)), dma((2, 2)), dma]
         )
@@ -469,10 +492,10 @@
         down_mate = over(far[2])
         up = placed(1, up, halves(far[1], up_mate))
         for layer in range(1, layers):
-            far, down_mate, up = after(far, 2 + layer, down_mate, up)
-            next_mate = over(far[2 + layer])
+            far, down_mate, up = after(far, 1 + layer, down_mate, up)
             down = placed(2, down, halves(far[1 + layer], down_mate, layer - 1))
-            down_mate = next_mate
+            far, down, up = after(far, 2 + layer, down, up)
+            down_mate = over(far[2 + layer])
         down = placed(2, down, halves(far[1 + layers], (), layers - 1))
         down = placed(2, down, [(one, True, h, layers - 1) for h, one in enumerate(down_mate)])
 

time: 492 us -> 490 us (level)
  no operation moved by 1% of the time
where the time goes in v3:
time: 490 us; the launch traced here: 488 us
  Pallas kernels  456 us (93%)
  starting transfers between devices  15.5 us (3%)
  waiting for transfers between devices  15.4 us (3%)
    pallas_call x1, Pallas kernels, update(): pl.pallas_call(functools.partial(kernel, dims, layers, n), out_shape=out_...  391 us
    pallas_call x7, Pallas kernels, moves(): pl.pallas_call(body, in_specs=[hbm] * (count + extra), out_specs=[hbm] *...  64.9 us
    ppermute x16, starting transfers between devices, moved(): return lax.ppermute(one, 'dp', list(enumerate(to)))  15.5 us
    ppermute x16, waiting for transfers between devices, moved(): return lax.ppermute(one, 'dp', list(enumerate(to)))  15.4 us
  transfers between devices with their start and end apart: 16, of which 3 were waited for; matrix products, arithmetic and copies ran while one was open for 0% of the time, Pallas kernels for 13%

profile of v3, /device:TPU:113, one launch (start us, length us, event | category | flops | bytes accessed | tf_op | source)
XLA Modules:
  0.0 487.9 jit_solution(10280199176007607080)
XLA Ops:
  0.6 391.2 %step.1 = (bf16[2,4,2,2,48,6144]{5,4,3,2,1,0:T(8,128)(2,1)}, bf16[2,4,2,2,48,6144]{5,4,3,2,1,0:T(8,128)(2,1)}, bf16[2,4,2,2,384,768]{5,4,3,2,1,0:T(8,128)(2,1)},...) custom-call(bf16[2,4,2,2,48,6144]{5,4,3,2,1,0:T(8,128)(2,1)} %bitcas, ...), custom_call_target="tpu_custom_call" | custom-call | tf_op jit(solution)/shard_map/step/pallas_call | solution.py:399
  391.9 0.1 collective-permute-start.4
  392.0 2.6 collective-permute-start.5
  394.7 0.0 collective-permute-start.2
  394.7 2.7 collective-permute-start.3
  397.3 32.0 %shard_map.187 = (bf16[2,4,2,2,48,6144]{5,4,3,2,1,0:T(8,128)(2,1)}, bf16[2,4,2,2,48,6144]{5,4,3,2,1,0:T(8,128)(2,1)}, f32[2,2,48,6144]{3,2,1,0:T(8,128)}, f32[2,...) custom-call(bf16[2,4,2,2,48,6144]{5,4,3,2,1,0:T(8,128)(2,1)} %get-tuple-element.68.refs_0_, ...), custom_call_target="tpu_custom_call" | custom-call | flops 754974720 | bytes 94371840 | tf_op jit(solution)/shard_map/pallas_call | solution.py:327
  429.3 0.0 collective-permute-done.4.refs_0_
  429.3 0.0 collective-permute-done.5.refs_1_
  429.4 1.3 collective-permute-start.6
  430.7 0.1 collective-permute-start.7
  430.8 16.8 %shard_map.188 = (bf16[2,4,2,2,384,768]{5,4,3,2,1,0:T(8,128)(2,1)}, f32[2,2,384,768]{3,2,1,0:T(8,128)}, f32[2,2,384,768]{3,2,1,0:T(8,128)}) custom-call(bf16[2,4,2,2,384,768]{5,4,3,2,1,0:T(8,128)(2,1)} %get-tuple-element.82.refs_0_, f32[2,2,384,768]{3,2,1,0:T(8,128)} %get-tuple-element.83.refs_1_, f32[2,2,384,768]{3,2,1,0:T(8,128)} %get-tuple-element.84.refs_2_, ...), custom_call_target="tpu_custom_call" | custom-call | flops 377487360 | bytes 47185920 | tf_op jit(solution)/shard_map/pallas_call | solution.py:327
  447.6 0.0 collective-permute-done.2.refs_0_
  447.6 0.0 collective-permute-done.3.refs_1_
  447.6 0.5 collective-permute-start.8
  448.1 0.1 collective-permute-start.9
  448.2 0.0 collective-permute-start
  448.2 2.7 collective-permute-start.1
  450.9 4.6 shard_map.189
  455.5 8.7 %collective-permute-done.refs_0_ = bf16[384,768]{1,0:T(8,128)(2,1)} collective-permute-done((bf16[384,768]{1,0:T(8,128)(2,1)}, bf16[384,768]{1,0:T(8,128)(2,1)}, u32[]{:S(2)}, u32[]{:S(2)}) %collective-permute-start) | collective-permute-done | bytes 589856 | tf_op jit(solution)/shard_map/ppermute | solution.py:413
  464.2 0.0 collective-permute-done.9.refs_3_
  464.2 1.3 collective-permute-start.12
  465.6 0.1 collective-permute-start.13
  465.7 2.7 collective-permute-start.11
  468.3 4.6 shard_map.190
  473.0 2.6 shard_map.191.refs_2_
  475.6 6.0 %collective-permute-done.10.refs_0_ = bf16[384,768]{1,0:T(8,128)(2,1)} collective-permute-done((bf16[384,768]{1,0:T(8,128)(2,1)}, bf16[384,768]{1,0:T(8,128)(2,1)}, u32[]{:S(2)}, u32[]{:S(2)}) %collective-permute-start.10) | collective-permute-done | bytes 589856 | tf_op jit(solution)/shard_map/ppermute | solution.py:413
  481.7 0.0 collective-permute-done.11.refs_1_
  481.7 1.3 collective-permute-start.14
  482.9 0.0 collective-permute-start.15
  482.9 2.1 shard_map.192.refs_2_
  485.1 0.7 collective-permute-done.15.refs_1_
  485.8 2.1 shard_map.193
  (8 shorter events, 0.0 us)
Async XLA Ops:
  391.9 37.4 %collective-permute-start.4 = (bf16[2,48,6144]{2,1,0:T(8,128)(2,1)}, bf16[2,48,6144]{2,1,0:T(8,128)(2,1)}, u32[]{:S(2)}, u32[]{:S(2)}) collective-permute-start(bf16[2,48,6144]{2,1,0:T(8,128)(2,1)} %get-tuple-element.66.refs_6_), channel_id=1, source_target_pairs={{0,2},{1,3},{2,4},{3,5},{4,6},{5,7},{6,0},{7,1},{8,10},{9,11},{10,... | collective-permute-start | bytes 3538952 | tf_op jit(solution)/shard_map/ppermute | solution.py:413
  392.0 37.3 %collective-permute-start.5 = (bf16[2,48,6144]{2,1,0:T(8,128)(2,1)}, bf16[2,48,6144]{2,1,0:T(8,128)(2,1)}, u32[]{:S(2)}, u32[]{:S(2)}) collective-permute-start(bf16[2,48,6144]{2,1,0:T(8,128)(2,1)} %get-tuple-element.67.refs_7_), channel_id=1, source_target_pairs={{0,6},{1,7},{2,0},{3,1},{4,2},{5,3},{6,4},{7,5},{8,14},{9,15},{10,... | collective-permute-start | bytes 3538952 | tf_op jit(solution)/shard_map/ppermute | solution.py:413
  394.7 52.9 %collective-permute-start.2 = (bf16[2,48,6144]{2,1,0:T(8,128)(2,1)}, bf16[2,48,6144]{2,1,0:T(8,128)(2,1)}, u32[]{:S(2)}, u32[]{:S(2)}) collective-permute-start(bf16[2,48,6144]{2,1,0:T(8,128)(2,1)} %get-tuple-element.64.refs_8_), channel_id=1, source_target_pairs={{0,2},{1,3},{2,4},{3,5},{4,6},{5,7},{6,0},{7,1},{8,10},{9,11},{10,... | collective-permute-start | bytes 3538952 | tf_op jit(solution)/shard_map/ppermute | solution.py:413
  394.7 52.9 %collective-permute-start.3 = (bf16[2,48,6144]{2,1,0:T(8,128)(2,1)}, bf16[2,48,6144]{2,1,0:T(8,128)(2,1)}, u32[]{:S(2)}, u32[]{:S(2)}) collective-permute-start(bf16[2,48,6144]{2,1,0:T(8,128)(2,1)} %get-tuple-element.65.refs_9_), channel_id=1, source_target_pairs={{0,6},{1,7},{2,0},{3,1},{4,2},{5,3},{6,4},{7,5},{8,14},{9,15},{10,... | collective-permute-start | bytes 3538952 | tf_op jit(solution)/shard_map/ppermute | solution.py:413
  429.4 18.3 %collective-permute-start.6 = (bf16[2,48,6144]{2,1,0:T(8,128)(2,1)}, bf16[2,48,6144]{2,1,0:T(8,128)(2,1)}, u32[]{:S(2)}, u32[]{:S(2)}) collective-permute-start(bf16[2,48,6144]{2,1,0:T(8,128)(2,1)} %collective-permute-done.4.refs_0_), channel_id=1, source_target_pairs={{0,1},{1,0},{2,3},{3,2},{4,5},{5,4},{6,7},{7,6},{8,9},{9,8},{10,11... | collective-permute-start | bytes 3538952 | tf_op jit(solution)/shard_map/ppermute | solution.py:413
  430.7 16.9 %collective-permute-start.7 = (bf16[2,48,6144]{2,1,0:T(8,128)(2,1)}, bf16[2,48,6144]{2,1,0:T(8,128)(2,1)}, u32[]{:S(2)}, u32[]{:S(2)}) collective-permute-start(bf16[2,48,6144]{2,1,0:T(8,128)(2,1)} %collective-permute-done.5.refs_1_), channel_id=1, source_target_pairs={{0,1},{1,0},{2,3},{3,2},{4,5},{5,4},{6,7},{7,6},{8,9},{9,8},{10,11... | collective-permute-start | bytes 3538952 | tf_op jit(solution)/shard_map/ppermute | solution.py:413
  447.6 16.6 %collective-permute-start.8 = (bf16[2,48,6144]{2,1,0:T(8,128)(2,1)}, bf16[2,48,6144]{2,1,0:T(8,128)(2,1)}, u32[]{:S(2)}, u32[]{:S(2)}) collective-permute-start(bf16[2,48,6144]{2,1,0:T(8,128)(2,1)} %collective-permute-done.2.refs_0_), channel_id=1, source_target_pairs={{0,1},{1,0},{2,3},{3,2},{4,5},{5,4},{6,7},{7,6},{8,9},{9,8},{10,11... | collective-permute-start | bytes 3538952 | tf_op jit(solution)/shard_map/ppermute | solution.py:413
  448.1 16.1 %collective-permute-start.9 = (bf16[2,48,6144]{2,1,0:T(8,128)(2,1)}, bf16[2,48,6144]{2,1,0:T(8,128)(2,1)}, u32[]{:S(2)}, u32[]{:S(2)}) collective-permute-start(bf16[2,48,6144]{2,1,0:T(8,128)(2,1)} %collective-permute-done.3.refs_1_), channel_id=1, source_target_pairs={{0,1},{1,0},{2,3},{3,2},{4,5},{5,4},{6,7},{7,6},{8,9},{9,8},{10,11... | collective-permute-start | bytes 3538952 | tf_op jit(solution)/shard_map/ppermute | solution.py:413
  448.2 16.0 %collective-permute-start = (bf16[384,768]{1,0:T(8,128)(2,1)}, bf16[384,768]{1,0:T(8,128)(2,1)}, u32[]{:S(2)}, u32[]{:S(2)}) collective-permute-start(bf16[384,768]{1,0:T(8,128)(2,1)} %get-tuple-element.85.refs_3_), channel_id=1, source_target_pairs={{0,2},{1,3},{2,4},{3,5},{4,6},{5,7},{6,0},{7,1},{8,10},{9,11},{10,... | collective-permute-start | bytes 1769480 | tf_op jit(solution)/shard_map/ppermute | solution.py:413
  448.2 16.0 %collective-permute-start.1 = (bf16[384,768]{1,0:T(8,128)(2,1)}, bf16[384,768]{1,0:T(8,128)(2,1)}, u32[]{:S(2)}, u32[]{:S(2)}) collective-permute-start(bf16[384,768]{1,0:T(8,128)(2,1)} %get-tuple-element.86.refs_4_), channel_id=1, source_target_pairs={{0,6},{1,7},{2,0},{3,1},{4,2},{5,3},{6,4},{7,5},{8,14},{9,15},{10,... | collective-permute-start | bytes 1769480 | tf_op jit(solution)/shard_map/ppermute | solution.py:413
  464.2 8.8 %collective-permute-start.12 = (bf16[384,768]{1,0:T(8,128)(2,1)}, bf16[384,768]{1,0:T(8,128)(2,1)}, u32[]{:S(2)}, u32[]{:S(2)}) collective-permute-start(bf16[384,768]{1,0:T(8,128)(2,1)} %collective-permute-done.refs_0_), channel_id=1, source_target_pairs={{0,1},{1,0},{2,3},{3,2},{4,5},{5,4},{6,7},{7,6},{8,9},{9,8},{10,11... | collective-permute-start | bytes 1769480 | tf_op jit(solution)/shard_map/ppermute | solution.py:413
  465.6 7.4 %collective-permute-start.13 = (bf16[384,768]{1,0:T(8,128)(2,1)}, bf16[384,768]{1,0:T(8,128)(2,1)}, u32[]{:S(2)}, u32[]{:S(2)}) collective-permute-start(bf16[384,768]{1,0:T(8,128)(2,1)} %collective-permute-done.1.refs_1_), channel_id=1, source_target_pairs={{0,1},{1,0},{2,3},{3,2},{4,5},{5,4},{6,7},{7,6},{8,9},{9,8},{10,11... | collective-permute-start | bytes 1769480 | tf_op jit(solution)/shard_map/ppermute | solution.py:413
  465.7 16.0 %collective-permute-start.10 = (bf16[384,768]{1,0:T(8,128)(2,1)}, bf16[384,768]{1,0:T(8,128)(2,1)}, u32[]{:S(2)}, u32[]{:S(2)}) collective-permute-start(bf16[384,768]{1,0:T(8,128)(2,1)} %get-tuple-element.87.refs_5_), channel_id=1, source_target_pairs={{0,2},{1,3},{2,4},{3,5},{4,6},{5,7},{6,0},{7,1},{8,10},{9,11},{10,... | collective-permute-start | bytes 1769480 | tf_op jit(solution)/shard_map/ppermute | solution.py:413
  465.7 16.0 %collective-permute-start.11 = (bf16[384,768]{1,0:T(8,128)(2,1)}, bf16[384,768]{1,0:T(8,128)(2,1)}, u32[]{:S(2)}, u32[]{:S(2)}) collective-permute-start(bf16[384,768]{1,0:T(8,128)(2,1)} %get-tuple-element.88.refs_6_), channel_id=1, source_target_pairs={{0,6},{1,7},{2,0},{3,1},{4,2},{5,3},{6,4},{7,5},{8,14},{9,15},{10,... | collective-permute-start | bytes 1769480 | tf_op jit(solution)/shard_map/ppermute | solution.py:413
  481.7 3.4 collective-permute-start.14
  482.9 2.8 collective-permute-start.15

commit v4 on v3

--- a/solution.py
+++ b/solution.py
@@ -27,7 +27,7 @@
     return (w - 0.02 * step).astype(jnp.bfloat16), m, v
 
 
-def kernel(dims, layers, n, *refs):
+def kernel(dims, layers, n, groups, *refs):
     kinds = 2
     it = iter(refs)
 
@@ -36,7 +36,8 @@
 
     g, w, m, v = take(3), take(3), take(3), take(3)
     w_out, m_out, v_out = take(3), take(3), take(3)
-    of_left, of_right = take(2 + layers), take(2 + layers)
+    of_left, of_right = take(len(groups)), take(len(groups))
+    kept = take(2)
     pair, hop1, hop2 = take(3), take(3), take(3)
     own, other, r1, r2, s1, s2, mb, vb, wb = (take(kinds) for _ in range(9))
     (pair_r, hop1_r, hop2_r, near_r, core_r, open_r) = take(6)
@@ -71,13 +72,17 @@
     def near(t, f):
         def go(W, k, l, p):
             if W < 2:
-                f(W, l, p, of_left[W].at[l, *p], of_right[W].at[l, *p])
+                f(W, l, p, W, (l, *p))
                 return
-            for layer in range(layers):
-
-                @pl.when(l == layer)
-                def _():
-                    f(W, layer, p, of_left[2 + layer].at[*p], of_right[2 + layer].at[*p])
+            height = dims[W][0] // SUB
+            j = (t - W * per) % SUB
+            for number, group in enumerate(groups):
+                if group is not None:
+                    layer, begin, end = group
+
+                    @pl.when((l == layer) & (j >= begin) & (j < end))
+                    def _():
+                        f(W, layer, p, number, (pl.ds(pl.multiple_of((j - begin) * height, 16), height), slice(None)))
 
         at(t, go)
 
@@ -232,22 +237,25 @@
         at(t, go)
 
     def spread(t):
-        def go(W, l, p, from_left, from_right):
+        def go(W, l, p, number, place):
             mine, first, last = w_out[W].at[l, x, c, :, *p], w_out[W].at[l, x, c, 0, *p], w_out[W].at[l, x, c, 1, *p]
-            remote(first, from_left, near_s.at[W], near_r.at[t], right).start()
-            remote(last, from_right, near_s.at[W], near_r.at[t], left).start()
-            remote(last, last, near_s.at[W], near_r.at[t], right).start()
-            remote(first, first, near_s.at[W], near_r.at[t], left).start()
+            final = number == len(groups) - 1
+            remote(first, of_left[number].at[*place], near_s.at[W], near_r.at[t], right).start()
+            remote(last, of_right[number].at[*place], near_s.at[W], near_r.at[t], left).start()
+            remote(last, kept[0].at[*place] if final else last, near_s.at[W], near_r.at[t], right).start()
+            remote(first, kept[1].at[*place] if final else first, near_s.at[W], near_r.at[t], left).start()
             remote(mine, mine, near_s.at[W], core_r.at[W], mate).start()
 
         near(t, go)
 
     def relay(t):
-        def go(W, l, p, from_left, from_right):
+        def go(W, l, p, number, place):
             landed(hop2[W].at[l, :, :, *p], near_r.at[t])
+            if number == len(groups) - 1:
+                return
             left0, left1 = w_out[W].at[l, lx, c, 0, *p], w_out[W].at[l, lx, c, 1, *p]
             right0, right1 = w_out[W].at[l, rx, c, 0, *p], w_out[W].at[l, rx, c, 1, *p]
-            for src, dst in ((from_left, left0), (left1, left1), (right0, right0), (from_right, right1)):
+            for src, dst in ((of_left[number].at[*place], left0), (left1, left1), (right0, right0), (of_right[number].at[*place], right1)):
                 remote(src, dst, last_s.at[W], core_r.at[W], mate).start()
 
         near(t, go)
@@ -281,14 +289,20 @@
         landed(mb[1].at[t % 2], mv_w.at[t % 2, 0])
         landed(vb[1].at[t % 2], mv_w.at[t % 2, 1])
     for W in range(3):
-        landed(w_out[W].at[:, pl.ds(0, 3), 0], core_r.at[W])
+        final = 0 if W < 2 else groups[-1][2] - groups[-1][1]
         landed(pair[W], pair_s.at[W])
         landed(w_out[W].at[:, pl.ds(0, 3), 0], near_s.at[W])
-        landed(w_out[W].at[:, pl.ds(0, 2), 0], last_s.at[W])
-
-
-def moves(sources, results, jobs, given=None):
-    count, extra = len(sources), 0 if given is None else 1
+        if W < 2:
+            landed(w_out[W].at[:, pl.ds(0, 3), 0], core_r.at[W])
+            landed(w_out[W].at[:, pl.ds(0, 2), 0], last_s.at[W])
+        else:
+            for sem, count in ((core_r, 3 * per - 2 * final), (last_s, 2 * per - 2 * final)):
+                rows = count * (dims[W][0] // SUB) // (layers * chips)
+                landed(pair[W].at[:, :, :, pl.ds(0, rows)], sem.at[W])
+
+
+def moves(sources, results, jobs, given=()):
+    count, extra = len(sources), len(given)
 
     def body(*refs):
         ins, outs = refs[:count], refs[count + extra : count + extra + len(results)]
@@ -331,10 +345,10 @@
         out_shape=results,
         scratch_shapes=[pltpu.VMEM((job[3], *job[5]), sources[job[0]].dtype) for job in jobs]
         + [pltpu.SemaphoreType.DMA((len(jobs), most))] * 2,
-        input_output_aliases={count: 0} if extra else {},
+        input_output_aliases={count + i: i for i in range(extra)},
         compiler_params=pltpu.CompilerParams(vmem_limit_bytes=VMEM),
         cost_estimate=pl.CostEstimate(flops=nbytes * 8, bytes_accessed=nbytes, transcendentals=0),
-    )(*sources, *(() if given is None else (given,)))
+    )(*sources, *given)
 
 
 def solution(mesh):
@@ -363,12 +377,16 @@
         def outs(*lead, dtype=BF16):
             return [jax.ShapeDtypeStruct((*lead, *dims[W]), dtype) for W in range(3)]
 
-        nears = outs(layers)[:2] + [jax.ShapeDtypeStruct(dims[2], BF16)] * layers
+        cuts = [(l, 0, SUB) for l in range(layers)]
+        groups = [None, None] + cuts
+        high = dims[2][0] // SUB
+        nears = outs(layers)[:2] + [jax.ShapeDtypeStruct(((end - begin) * high, dims[2][1]), BF16) for _, begin, end in cuts]
         out_shape = (
             outs(layers, chips, CORES, HALVES)
             + outs(layers, HALVES, dtype=F32)
             + outs(layers, HALVES, dtype=F32)
             + nears * 2
+            + nears[-1:] * 2
             + outs(layers, chips, HALVES)
             + outs(layers, 2)
             + outs(layers, 2, HALVES)
@@ -397,7 +415,7 @@
         )
         hbm = pl.BlockSpec(memory_space=pltpu.HBM)
         result = pl.pallas_call(
-            functools.partial(kernel, dims, layers, n),
+            functools.partial(kernel, dims, layers, n, groups),
             out_shape=out_shape,
             in_specs=[hbm] * len(inputs),
             out_specs=[hbm] * len(out_shape),
@@ -407,6 +425,7 @@
         )(*inputs)
         new_w, new_m, new_v = result[:3], result[3:6], result[6:9]
         of_left, of_right = result[9 : 9 + len(nears)], result[9 + len(nears) : 9 + 2 * len(nears)]
+        kept = result[9 + 2 * len(nears) :][:2]
 
         def moved(one, along, other=False):
             to = [((d // CORES + along) % chips * CORES + (d % CORES + other) % CORES) for d in range(n)]
@@ -417,26 +436,33 @@
 
         every = slice(None)
 
-        def of_blocks(W, src, dst, blocks, half, slots, ahead):
+        def of_blocks(W, src, dst, blocks, half, slots, ahead, spans=None):
+            spans = spans or [(l, dims[W][0]) for l in range(layers)]
+
             def where(i, x, c):
-                along, other, which = blocks[i // layers]
-                place = (i % layers, (x + along) % chips, 1 - c if other else c, which)
+                along, other, which = blocks[i // len(spans)]
+                l, rows = spans[i % len(spans)]
+                place = (l, (x + along) % chips, 1 - c if other else c, which, slice(0, rows))
                 return place, place
 
-            return src, dst, layers * len(blocks), slots, ahead, dims[W] if half else (HALVES, *dims[W]), where
-
-        def of_near(W, src, dst, along, other, half, layer=None, slots=2):
-            cuts = 2
-            shape = (dims[W][0], dims[W][1] // cuts) if W < 2 else (dims[W][0] // cuts, dims[W][1])
+            shape = (spans[0][1], dims[W][1])
+            return src, dst, len(spans) * len(blocks), slots, ahead, shape if half else (HALVES, *shape), where
+
+        def of_near(number, src, dst, along, other, half, slots=4):
+            W, parts = min(number, 2), 2
+            l, begin, end = groups[number] or (None, 0, SUB)
+            height = (end - begin) * dims[W][0] // SUB
+            shape = (height, dims[W][1] // parts) if W < 2 else (height // parts, dims[W][1])
 
             def where(i, x, c):
-                q = i % cuts
-                at = (every, pl.ds(q * shape[1], shape[1])) if W < 2 else (pl.ds(q * shape[0], shape[0]), every)
-                l = i // cuts if layer is None else layer
-                return ((l, *at) if layer is None else at), (l, (x + along) % chips, 1 - c if other else c, half, *at)
-
-            steps = cuts * (layers if layer is None else 1)
-            return src, dst, steps, slots, slots // 2, shape, where
+                q = i % parts
+                to = ((x + along) % chips, 1 - c if other else c, half)
+                if W < 2:
+                    at = (every, pl.ds(q * shape[1], shape[1]))
+                    return (i // parts, *at), (i // parts, *to, *at)
+                return (pl.ds(q * shape[0], shape[0]), every), (l, *to, pl.ds(begin * high + q * shape[0], shape[0]), every)
+
+            return src, dst, parts * (layers if W < 2 else 1), slots, slots // 2, shape, where
 
         def of_moment(W, src, dst, cuts, slots, ahead):
             shape = (dims[W][0], dims[W][1] // cuts) if W < 2 else (dims[W][0] // cuts, dims[W][1])
@@ -449,30 +475,39 @@
 
             return src, dst, layers * HALVES * cuts, slots, ahead, shape, where
 
-        def copied(which, new_w, new_m, new_v, of_left, of_right):
+        def copied(which, new_w, new_m, new_v, of_left, of_right, held=()):
             here = [one[W] for one in (new_w, new_m, new_v) for W in which]
             count, jobs, late = len(which), [], []
             for q, W in enumerate(which):
-                full = ((0, False, every), (0, True, every), (-1, True, every), (1, True, every))
-                jobs.append(of_blocks(W, q, q, full, False, 6, 3))
-                jobs.append(of_blocks(W, q, q, ((-1, False, 1), (1, False, 0)), True, 4, 2))
+                own, beside = ((0, False, every), (0, True, every)), ((-1, True, every), (1, True, every))
+                if W < 2:
+                    jobs.append(of_blocks(W, q, q, own + beside, False, 6, 3))
+                    jobs.append(of_blocks(W, q, q, ((-1, False, 1), (1, False, 0)), True, 4, 2))
+                else:
+                    jobs.append(of_blocks(W, q, q, own, False, 4, 2))
+                    for span in [(l, dims[W][0]) for l in range(layers - 1)]:
+                        jobs.append(of_blocks(W, q, q, beside, False, 2, 2, [span]))
+                        jobs.append(of_blocks(W, q, q, ((-1, False, 1), (1, False, 0)), True, 2, 2, [span]))
                 jobs += [of_moment(W, i, i, 2, 6, 3) for i in (count + q, 2 * count + q)]
-                for layer in (None,) if W < 2 else range(layers):
-                    at = W + (layer or 0)
+                for number in (W,) if W < 2 else range(2, len(groups)):
                     for one, along, half in ((of_left, -1, 0), (of_right, 1, 1)):
-                        jobs.append(of_near(W, len(here) + len(late), q, along, False, half, layer, 4))
-                        late.append(one[at])
+                        jobs.append(of_near(number, len(here) + len(late), q, along, False, half))
+                        late.append(one[number])
+                for one, place in held:
+                    jobs.append(of_near(len(groups) - 1, len(here) + len(late), q, *place))
+                    late.append(one)
             return moves((*here, *late), [like(one) for one in here], jobs)
 
-        def placed(W, one, halves):
-            jobs = [of_near(W, i, 0, 2, other, half, layer, 4) for i, (_, other, half, layer) in enumerate(halves)]
-            return moves([half[0] for half in halves], [like(one)], jobs, one)[0]
+        def placed(given, halves):
+            low = min(min(number, 2) for _, number, _, _ in halves)
+            jobs = [of_near(number, i, min(number, 2) - low, 2, other, half) for i, (_, number, other, half) in enumerate(halves)]
+            return moves([half[0] for half in halves], [like(one) for one in given], jobs, given)
 
         def over(far):
             return [moved(one, 0, True) for one in far]
 
-        def halves(far, mates, layer=None):
-            return [(one, other, h, layer) for other, both in ((False, far), (True, mates)) for h, one in enumerate(both)]
+        def halves(both, number, other):
+            return [(one, number, other, h) for h, one in enumerate(both)]
 
         def after(far, which, *others):
             one, others = lax.optimization_barrier((far[which], others))
@@ -481,23 +516,26 @@
         far = []
         for a, b in zip(of_left, of_right, strict=True):
             far.append((moved(a, 1), moved(b, -1)))
+        last = len(groups) - 1
+        ones = over((of_left[last], kept[0], kept[1], of_right[last]))
         gate, up, gate_m, up_m, gate_v, up_v = copied((0, 1), new_w, new_m, new_v, of_left, of_right)
-        far, _, *rest = after(far, 0, gate_m, new_w, new_m, new_v, of_left, of_right)
+        far, _, ones, *rest = after(far, 0, gate_m, ones, new_w, new_m, new_v, of_left, of_right)
         gate_mate = over(far[0])
-        down, down_m, down_v = copied((2,), *rest)
+        held = [(one, (along, True, h)) for one, along, h in zip(ones, (-1, -1, 1, 1), (0, 1, 0, 1), strict=True)]
+        held += [(kept[0], (-1, False, 1)), (kept[1], (1, False, 0))]
+        down, down_m, down_v = copied((2,), *rest, held)
         far, gate_mate, _ = after(far, 1, gate_mate, down_m)
         up_mate = over(far[1])
-        gate = placed(0, gate, halves(far[0], gate_mate))
-        far, up_mate, gate = after(far, 2, up_mate, gate)
-        down_mate = over(far[2])
-        up = placed(1, up, halves(far[1], up_mate))
-        for layer in range(1, layers):
-            far, down_mate, up = after(far, 1 + layer, down_mate, up)
-            down = placed(2, down, halves(far[1 + layer], down_mate, layer - 1))
-            far, down, up = after(far, 2 + layer, down, up)
-            down_mate = over(far[2 + layer])
-        down = placed(2, down, halves(far[1 + layers], (), layers - 1))
-        down = placed(2, down, [(one, True, h, layers - 1) for h, one in enumerate(down_mate)])
+        far, gate_mate, up_mate = after(far, 2, gate_mate, up_mate)
+        mates = over(far[2])
+        gate, up = placed((gate, up), halves(far[0], 0, False) + halves(gate_mate, 0, True) + halves(far[1], 1, False) + halves(up_mate, 1, True))
+        for number in range(3, len(groups)):
+            mates, up = lax.optimization_barrier((mates, up))
+            (down,) = placed((down,), halves(far[number - 1], number - 1, False) + halves(mates, number - 1, True))
+            far, down, up = after(far, number, down, up)
+            mates = over(far[number])
+        (down,) = placed((down,), halves(far[last], last, False))
+        (down,) = placed((down,), halves(mates, last, True))
 
         found = (gate, up, down, gate_m, up_m, down_m, gate_v, up_v, down_v)
         return tuple(one.reshape(ref.shape) for one, ref in zip(found, (*weights, *m, *v), strict=True))

time: 490 us -> 498 us (1.016)
  waiting for transfers between devices: 15.4 us -> 25.2 us
    ppermute x16 -> x20, waiting for transfers between devices: 15.4 us -> 25.2 us  [moved(): return lax.ppermute(one, 'dp', list(enumerate(to)))]
    ppermute x16 -> x20, starting transfers between devices: 15.5 us -> 16.6 us  [moved(): return lax.ppermute(one, 'dp', list(enumerate(to)))]
    pallas_call x7 -> x6, Pallas kernels: 64.9 us -> 64.4 us  [moves(): pl.pallas_call(body, in_specs=[hbm] * (count + extra), out_specs=[hbm] *...]
  transfers between devices with their start and end apart: 16 -> 20, of which waited for: 3 -> 4; matrix products, arithmetic and copies ran while one was open for 0% -> 0% of each run, Pallas kernels for 13% -> 13%
where the time goes in v4:
time: 498 us; the launch traced here: 496 us
  Pallas kernels  453 us (91%)
  waiting for transfers between devices  25.2 us (5%)
  starting transfers between devices  16.6 us (3%)
    pallas_call x1, Pallas kernels, update(): pl.pallas_call(functools.partial(kernel, dims, layers, n, groups), out_sh...  389 us
    pallas_call x6, Pallas kernels, moves(): pl.pallas_call(body, in_specs=[hbm] * (count + extra), out_specs=[hbm] *...  64.4 us
    ppermute x20, waiting for transfers between devices, moved(): return lax.ppermute(one, 'dp', list(enumerate(to)))  25.2 us
    ppermute x20, starting transfers between devices, moved(): return lax.ppermute(one, 'dp', list(enumerate(to)))  16.6 us
  transfers between devices with their start and end apart: 20, of which 4 were waited for; matrix products, arithmetic and copies ran while one was open for 0% of the time, Pallas kernels for 13%

profile of v4, /device:TPU:113, one launch (start us, length us, event | category | flops | bytes accessed | tf_op | source)
XLA Modules:
  0.0 495.8 jit_solution(15778351984854484595)
XLA Ops:
  0.6 388.8 %step.1 = (bf16[2,4,2,2,48,6144]{5,4,3,2,1,0:T(8,128)(2,1)}, bf16[2,4,2,2,48,6144]{5,4,3,2,1,0:T(8,128)(2,1)}, bf16[2,4,2,2,384,768]{5,4,3,2,1,0:T(8,128)(2,1)},...) custom-call(bf16[2,4,2,2,48,6144]{5,4,3,2,1,0:T(8,128)(2,1)} %bitcas, ...), custom_call_target="tpu_custom_call" | custom-call | tf_op jit(solution)/shard_map/step/pallas_call | solution.py:417
  389.5 0.6 collective-permute-start.2
  390.1 0.1 collective-permute-start
  390.2 2.6 collective-permute-start.1
  392.8 0.7 collective-permute-start.5
  393.5 0.0 collective-permute-done.2.refs_7_
  393.5 0.5 collective-permute-start.4
  394.0 32.0 %shard_map.187 = (bf16[2,4,2,2,48,6144]{5,4,3,2,1,0:T(8,128)(2,1)}, bf16[2,4,2,2,48,6144]{5,4,3,2,1,0:T(8,128)(2,1)}, f32[2,2,48,6144]{3,2,1,0:T(8,128)}, f32[2,...) custom-call(bf16[2,4,2,2,48,6144]{5,4,3,2,1,0:T(8,128)(2,1)} %get-tuple-element.71.refs_0_, ...), custom_call_target="tpu_custom_call" | custom-call | flops 754974720 | bytes 94371840 | tf_op jit(solution)/shard_map/pallas_call | solution.py:341
  426.0 0.0 collective-permute-done.5.refs_10_
  426.0 0.1 collective-permute-start.8
  426.1 0.0 collective-permute-done.3.refs_8_
  426.1 2.6 collective-permute-start.9
  428.8 0.3 collective-permute-start.10
  429.1 0.3 collective-permute-start.11
  429.4 17.8 %shard_map.188 = (bf16[2,4,2,2,384,768]{5,4,3,2,1,0:T(8,128)(2,1)}, f32[2,2,384,768]{3,2,1,0:T(8,128)}, f32[2,2,384,768]{3,2,1,0:T(8,128)}) custom-call(bf16[2,4,2,2,384,768]{5,4,3,2,1,0:T(8,128)(2,1)} %get-tuple-element.91.refs_0_, f32[2,2,384,768]{3,2,1,0:T(8,128)} %get-tuple-element.92.refs_1_, f32[2,2,384,768]{3,2,1,0:T(8,128)} %get-tuple-element.93.refs_2_, ...), custom_call_target="tpu_custom_call" | custom-call | flops 377487360 | bytes 47185920 | tf_op jit(solution)/shard_map/pallas_call | solution.py:341
  447.2 8.3 %collective-permute-done.8.refs_4_ = bf16[2,48,6144]{2,1,0:T(8,128)(2,1)} collective-permute-done((bf16[2,48,6144]{2,1,0:T(8,128)(2,1)}, bf16[2,48,6144]{2,1,0:T(8,128)(2,1)}, u32[]{:S(2)}, u32[]{:S(2)}) %collective-permute-start.8) | collective-permute-done | bytes 1179680 | tf_op jit(solution)/shard_map/ppermute | solution.py:432
  455.5 0.6 collective-permute-start.12
  456.1 0.1 collective-permute-start.13
  456.2 2.7 collective-permute-start.7
  458.9 13.3 %collective-permute-done.6.refs_0_ = bf16[384,768]{1,0:T(8,128)(2,1)} collective-permute-done((bf16[384,768]{1,0:T(8,128)(2,1)}, bf16[384,768]{1,0:T(8,128)(2,1)}, u32[]{:S(2)}, u32[]{:S(2)}) %collective-permute-start.6) | collective-permute-done | bytes 589856 | tf_op jit(solution)/shard_map/ppermute | solution.py:432
  472.2 1.3 collective-permute-start.16
  473.5 0.1 collective-permute-start.17
  473.6 0.7 collective-permute-start.14
  474.3 2.0 collective-permute-start.15
  476.3 7.8 %shard_map.189 = (bf16[2,4,2,2,48,6144]{5,4,3,2,1,0:T(8,128)(2,1)}, bf16[2,4,2,2,48,6144]{5,4,3,2,1,0:T(8,128)(2,1)}) custom-call(bf16[2,48,6144]{2,1,0:T(8,128)(2,1)} %collective-permute-done.refs_0_, bf16[2,48,6144]{2,1,0:T(8,128)(2,1)} %collective-permute-done.1.refs_1_, ...), custom_call_target="tpu_custom_call", output_to_operand_aliasing={{0}: (8, {}), {1}: (9, {})} | custom-call | flops 150994944 | bytes 18874368 | tf_op jit(solution)/shard_map/pallas_call | solution.py:341
  484.1 2.6 shard_map.190.refs_2_
  486.8 2.8 collective-permute-done.14.refs_0_
  489.6 1.3 collective-permute-start.18
  490.9 0.0 collective-permute-start.19
  490.9 2.1 shard_map.191.refs_2_
  493.0 0.7 collective-permute-done.19.refs_1_
  493.7 2.1 shard_map.192
  (15 shorter events, 0.0 us)
Async XLA Ops:
  389.5 4.0 collective-permute-start.2
  390.1 38.6 %collective-permute-start = (bf16[2,48,6144]{2,1,0:T(8,128)(2,1)}, bf16[2,48,6144]{2,1,0:T(8,128)(2,1)}, u32[]{:S(2)}, u32[]{:S(2)}) collective-permute-start(bf16[2,48,6144]{2,1,0:T(8,128)(2,1)} %get-tuple-element.69.refs_6_), channel_id=1, source_target_pairs={{0,2},{1,3},{2,4},{3,5},{4,6},{5,7},{6,0},{7,1},{8,10},{9,11},{10,... | collective-permute-start | bytes 3538952 | tf_op jit(solution)/shard_map/ppermute | solution.py:432
  390.2 38.6 %collective-permute-start.1 = (bf16[2,48,6144]{2,1,0:T(8,128)(2,1)}, bf16[2,48,6144]{2,1,0:T(8,128)(2,1)}, u32[]{:S(2)}, u32[]{:S(2)}) collective-permute-start(bf16[2,48,6144]{2,1,0:T(8,128)(2,1)} %get-tuple-element.70.refs_7_), channel_id=1, source_target_pairs={{0,6},{1,7},{2,0},{3,1},{4,2},{5,3},{6,4},{7,5},{8,14},{9,15},{10,... | collective-permute-start | bytes 3538952 | tf_op jit(solution)/shard_map/ppermute | solution.py:432
  392.8 33.2 %collective-permute-start.5 = (bf16[384,768]{1,0:T(8,128)(2,1)}, bf16[384,768]{1,0:T(8,128)(2,1)}, u32[]{:S(2)}, u32[]{:S(2)}) collective-permute-start(bf16[384,768]{1,0:T(8,128)(2,1)} %get-tuple-element.97.refs_6_), channel_id=1, source_target_pairs={{0,1},{1,0},{2,3},{3,2},{4,5},{5,4},{6,7},{7,6},{8,9},{9,8},{10,11... | collective-permute-start | bytes 1769480 | tf_op jit(solution)/shard_map/ppermute | solution.py:432
  393.5 32.6 %collective-permute-start.3 = (bf16[384,768]{1,0:T(8,128)(2,1)}, bf16[384,768]{1,0:T(8,128)(2,1)}, u32[]{:S(2)}, u32[]{:S(2)}) collective-permute-start(bf16[384,768]{1,0:T(8,128)(2,1)} %get-tuple-element.81.refs_11_), channel_id=1, source_target_pairs={{0,1},{1,0},{2,3},{3,2},{4,5},{5,4},{6,7},{7,6},{8,9},{9,8},{10,11... | collective-permute-start | bytes 1769480 | tf_op jit(solution)/shard_map/ppermute | solution.py:432
  393.5 35.3 %collective-permute-start.4 = (bf16[384,768]{1,0:T(8,128)(2,1)}, bf16[384,768]{1,0:T(8,128)(2,1)}, u32[]{:S(2)}, u32[]{:S(2)}) collective-permute-start(bf16[384,768]{1,0:T(8,128)(2,1)} %get-tuple-element.82.refs_12_), channel_id=1, source_target_pairs={{0,1},{1,0},{2,3},{3,2},{4,5},{5,4},{6,7},{7,6},{8,9},{9,8},{10,11... | collective-permute-start | bytes 1769480 | tf_op jit(solution)/shard_map/ppermute | solution.py:432
  426.0 29.5 %collective-permute-start.8 = (bf16[2,48,6144]{2,1,0:T(8,128)(2,1)}, bf16[2,48,6144]{2,1,0:T(8,128)(2,1)}, u32[]{:S(2)}, u32[]{:S(2)}) collective-permute-start(bf16[2,48,6144]{2,1,0:T(8,128)(2,1)} %get-tuple-element.77.refs_8_), channel_id=1, source_target_pairs={{0,2},{1,3},{2,4},{3,5},{4,6},{5,7},{6,0},{7,1},{8,10},{9,11},{10,... | collective-permute-start | bytes 3538952 | tf_op jit(solution)/shard_map/ppermute | solution.py:432
  426.1 29.3 %collective-permute-start.9 = (bf16[2,48,6144]{2,1,0:T(8,128)(2,1)}, bf16[2,48,6144]{2,1,0:T(8,128)(2,1)}, u32[]{:S(2)}, u32[]{:S(2)}) collective-permute-start(bf16[2,48,6144]{2,1,0:T(8,128)(2,1)} %get-tuple-element.78.refs_9_), channel_id=1, source_target_pairs={{0,6},{1,7},{2,0},{3,1},{4,2},{5,3},{6,4},{7,5},{8,14},{9,15},{10,... | collective-permute-start | bytes 3538952 | tf_op jit(solution)/shard_map/ppermute | solution.py:432
  428.8 26.7 %collective-permute-start.10 = (bf16[2,48,6144]{2,1,0:T(8,128)(2,1)}, bf16[2,48,6144]{2,1,0:T(8,128)(2,1)}, u32[]{:S(2)}, u32[]{:S(2)}) collective-permute-start(bf16[2,48,6144]{2,1,0:T(8,128)(2,1)} %collective-permute-done.refs_0_), channel_id=1, source_target_pairs={{0,1},{1,0},{2,3},{3,2},{4,5},{5,4},{6,7},{7,6},{8,9},{9,8},{10,11... | collective-permute-start | bytes 3538952 | tf_op jit(solution)/shard_map/ppermute | solution.py:432
  429.1 26.4 %collective-permute-start.11 = (bf16[2,48,6144]{2,1,0:T(8,128)(2,1)}, bf16[2,48,6144]{2,1,0:T(8,128)(2,1)}, u32[]{:S(2)}, u32[]{:S(2)}) collective-permute-start(bf16[2,48,6144]{2,1,0:T(8,128)(2,1)} %collective-permute-done.1.refs_1_), channel_id=1, source_target_pairs={{0,1},{1,0},{2,3},{3,2},{4,5},{5,4},{6,7},{7,6},{8,9},{9,8},{10,11... | collective-permute-start | bytes 3538952 | tf_op jit(solution)/shard_map/ppermute | solution.py:432
  455.5 16.7 %collective-permute-start.12 = (bf16[2,48,6144]{2,1,0:T(8,128)(2,1)}, bf16[2,48,6144]{2,1,0:T(8,128)(2,1)}, u32[]{:S(2)}, u32[]{:S(2)}) collective-permute-start(bf16[2,48,6144]{2,1,0:T(8,128)(2,1)} %collective-permute-done.8.refs_4_), channel_id=1, source_target_pairs={{0,1},{1,0},{2,3},{3,2},{4,5},{5,4},{6,7},{7,6},{8,9},{9,8},{10,11... | collective-permute-start | bytes 3538952 | tf_op jit(solution)/shard_map/ppermute | solution.py:432
  456.1 16.1 %collective-permute-start.13 = (bf16[2,48,6144]{2,1,0:T(8,128)(2,1)}, bf16[2,48,6144]{2,1,0:T(8,128)(2,1)}, u32[]{:S(2)}, u32[]{:S(2)}) collective-permute-start(bf16[2,48,6144]{2,1,0:T(8,128)(2,1)} %collective-permute-done.9.refs_5_), channel_id=1, source_target_pairs={{0,1},{1,0},{2,3},{3,2},{4,5},{5,4},{6,7},{7,6},{8,9},{9,8},{10,11... | collective-permute-start | bytes 3538952 | tf_op jit(solution)/shard_map/ppermute | solution.py:432
  456.2 16.0 %collective-permute-start.6 = (bf16[384,768]{1,0:T(8,128)(2,1)}, bf16[384,768]{1,0:T(8,128)(2,1)}, u32[]{:S(2)}, u32[]{:S(2)}) collective-permute-start(bf16[384,768]{1,0:T(8,128)(2,1)} %get-tuple-element.94.refs_3_), channel_id=1, source_target_pairs={{0,2},{1,3},{2,4},{3,5},{4,6},{5,7},{6,0},{7,1},{8,10},{9,11},{10,... | collective-permute-start | bytes 1769480 | tf_op jit(solution)/shard_map/ppermute | solution.py:432
  456.2 16.0 %collective-permute-start.7 = (bf16[384,768]{1,0:T(8,128)(2,1)}, bf16[384,768]{1,0:T(8,128)(2,1)}, u32[]{:S(2)}, u32[]{:S(2)}) collective-permute-start(bf16[384,768]{1,0:T(8,128)(2,1)} %get-tuple-element.95.refs_4_), channel_id=1, source_target_pairs={{0,6},{1,7},{2,0},{3,1},{4,2},{5,3},{6,4},{7,5},{8,14},{9,15},{10,... | collective-permute-start | bytes 1769480 | tf_op jit(solution)/shard_map/ppermute | solution.py:432
  472.2 11.9 %collective-permute-start.16 = (bf16[384,768]{1,0:T(8,128)(2,1)}, bf16[384,768]{1,0:T(8,128)(2,1)}, u32[]{:S(2)}, u32[]{:S(2)}) collective-permute-start(bf16[384,768]{1,0:T(8,128)(2,1)} %collective-permute-done.6.refs_0_), channel_id=1, source_target_pairs={{0,1},{1,0},{2,3},{3,2},{4,5},{5,4},{6,7},{7,6},{8,9},{9,8},{10,11... | collective-permute-start | bytes 1769480 | tf_op jit(solution)/shard_map/ppermute | solution.py:432
  473.5 10.6 %collective-permute-start.17 = (bf16[384,768]{1,0:T(8,128)(2,1)}, bf16[384,768]{1,0:T(8,128)(2,1)}, u32[]{:S(2)}, u32[]{:S(2)}) collective-permute-start(bf16[384,768]{1,0:T(8,128)(2,1)} %collective-permute-done.7.refs_1_), channel_id=1, source_target_pairs={{0,1},{1,0},{2,3},{3,2},{4,5},{5,4},{6,7},{7,6},{8,9},{9,8},{10,11... | collective-permute-start | bytes 1769480 | tf_op jit(solution)/shard_map/ppermute | solution.py:432
  473.6 16.0 %collective-permute-start.14 = (bf16[384,768]{1,0:T(8,128)(2,1)}, bf16[384,768]{1,0:T(8,128)(2,1)}, u32[]{:S(2)}, u32[]{:S(2)}) collective-permute-start(bf16[384,768]{1,0:T(8,128)(2,1)} %get-tuple-element.96.refs_5_), channel_id=1, source_target_pairs={{0,2},{1,3},{2,4},{3,5},{4,6},{5,7},{6,0},{7,1},{8,10},{9,11},{10,... | collective-permute-start | bytes 1769480 | tf_op jit(solution)/shard_map/ppermute | solution.py:432
  474.3 15.3 %collective-permute-start.15 = (bf16[384,768]{1,0:T(8,128)(2,1)}, bf16[384,768]{1,0:T(8,128)(2,1)}, u32[]{:S(2)}, u32[]{:S(2)}) collective-permute-start(bf16[384,768]{1,0:T(8,128)(2,1)} %get-tuple-element.97.refs_6_), channel_id=1, source_target_pairs={{0,6},{1,7},{2,0},{3,1},{4,2},{5,3},{6,4},{7,5},{8,14},{9,15},{10,... | collective-permute-start | bytes 1769480 | tf_op jit(solution)/shard_map/ppermute | solution.py:432
  489.6 3.4 collective-permute-start.18
  490.9 2.8 collective-permute-start.19
